TPU v7x, 32 devices: a whole 2x2x4 slice. The times are simulated.
32 devices in a mesh: rep: 2 (over x), ep: 8 (over z, y), tp: 2 (over core).
Axes of the slice: x: 2, y: 2, z: 4, core: 2. Of those that a mesh axis runs over, the one named last changes fastest.
Arguments:
- tokens: bfloat16 [1024, 3072], P(('rep', 'ep')), parts along dimension 0, may hold values from -6 to 6
- routes: int32 [1024, 2], P(('rep', 'ep')), parts along dimension 0, may hold values from 0 to 3, all different within a row; in each aligned block of 64 rows (0 to 63, 64 to 127, ...) at most 40 rows name the same one
- route_weight: float32 [1024, 2], P(('rep', 'ep')), parts along dimension 0, may hold values from 0.2 to 1
- gate_code: bfloat16 [3072, 32768], P(None, ('ep', 'tp')), may hold values from -0.109375 to 0.109375
- gate_scale: float32 [3072, 256], P(None, ('ep', 'tp')), may hold values from 0.5 to 2
- up_code: bfloat16 [3072, 32768], P(None, ('ep', 'tp')), may hold values from -0.109375 to 0.109375
- up_scale: float32 [3072, 256], P(None, ('ep', 'tp')), may hold values from 0.5 to 2
- down_code: bfloat16 [32768, 3072], P(('ep', 'tp')), may hold values from -0.0625 to 0.0625
- down_scale: float32 [32768, 24], P(('ep', 'tp')), may hold values from 0.5 to 2
Outputs:
- mixed: bfloat16 [1024, 3072], P(('rep', 'ep'), 'tp'), parts along dimension 0
There are 2 independent parts, one for each index of `rep`. A program takes and returns all parts, laid end to end along the dimension named above; an argument that names none is the same for every part. Nothing has to cross between parts.
Inputs may be any that keep to these rules, and one draw needn't show every extreme that they name: `routes`: among the 64 rows of one index of ep, no expert is named by more than 40 rows, a bound that some block reaches; a row names 2 different experts.
All inputs are finite; a program needn't handle non-finite values.
Results may differ from a plain program's by a relative error of at most 0.02.
Values may be sent and summed in bfloat16 or wider, within the bound.
No kernel may reach another device: no remote copies, remote signals or barrier semaphores. Data moves between devices by JAX's collectives and lax.ppermute only.
A program may use at most 128 MiB of HBM per device.

v0:
```python
import functools

import jax
import jax.numpy as jnp
from jax import lax
from jax.experimental import pallas as pl
from jax.experimental.pallas import tpu as pltpu
from jax.sharding import PartitionSpec as P

EXPERTS = 4
TOP = 2
QB = 128
CAP = 40
F32 = jnp.float32
BF16 = jnp.bfloat16
VMEM = pltpu.VMEM
MIB = 2**20


def whole():
    return pl.BlockSpec(memory_space=VMEM)


def scalar():
    return pl.BlockSpec(memory_space=pltpu.SMEM)


def ranks(routes_t, expert):
    count = routes_t.shape[1]
    named = (routes_t[0:1, :] == expert).astype(F32)
    for k in range(1, TOP):
        named = named + (routes_t[k : k + 1, :] == expert).astype(F32)
    rows = lax.broadcasted_iota(jnp.int32, (count, count), 0)
    cols = lax.broadcasted_iota(jnp.int32, (count, count), 1)
    earlier = (rows < cols).astype(F32)
    wide = jnp.broadcast_to(named, (8, count))
    return named, jnp.dot(wide, earlier, preferred_element_type=F32)[0:1, :]


def pack_kernel(place, routes_ref, tokens_ref, *outs):
    own = place[0]
    routes_t = routes_ref[...]
    count = routes_t.shape[1]
    slots = lax.broadcasted_iota(jnp.int32, (CAP, count), 0)
    for d, out in enumerate(outs):
        named, rank = ranks(routes_t, own ^ d)
        hit = (slots == rank.astype(jnp.int32)) & (jnp.broadcast_to(named, (CAP, count)) > 0.5)
        picked = jnp.where(hit, 1.0, 0.0).astype(BF16)
        out[...] = jnp.dot(picked, tokens_ref[...], preferred_element_type=F32).astype(BF16)


def pack(place, routes_t, tokens, parts):
    count, width = tokens.shape
    part = width // parts
    tokens = pltpu.with_memory_space_constraint(tokens, pltpu.HBM)
    return pl.pallas_call(
        pack_kernel,
        grid_spec=pltpu.PrefetchScalarGridSpec(
            num_scalar_prefetch=1,
            grid=(1,),
            in_specs=[
                pl.BlockSpec(routes_t.shape, lambda i, place: (0, 0)),
                pl.BlockSpec((count, part), lambda i, place: (0, place[1])),
            ],
            out_specs=[pl.BlockSpec((CAP, part), lambda i, place: (0, 0))] * EXPERTS,
        ),
        out_shape=[jax.ShapeDtypeStruct((CAP, part), BF16)] * EXPERTS,
        compiler_params=pltpu.CompilerParams(vmem_limit_bytes=4 * MIB),
        name="pack",
    )(place, routes_t, tokens)


def dequant_kernel(step, code, scale_hbm, out, sems, scale_sem, scale_ref, spread, split, column):
    rows, _ = out.shape
    blocks = scale_ref.shape[0]
    scale_copy = pltpu.make_async_copy(scale_hbm, scale_ref, scale_sem)
    scale_copy.start()
    copies = []
    for i in range(rows // step):
        at = pl.ds(i * step, step)
        copies.append(pltpu.make_async_copy(code.at[at], out.at[at], sems.at[i]))
    for copy in copies:
        copy.start()
    row = lax.broadcasted_iota(jnp.int32, spread.shape, 0)
    col = lax.broadcasted_iota(jnp.int32, spread.shape, 1)
    spread[...] = jnp.where(lax.rem(row, blocks) == lax.div(col, QB), 1.0, 0.0).astype(BF16)
    scale_copy.wait()
    scale = scale_ref[...]
    high = scale.astype(BF16).astype(F32)
    column[...] = scale.T
    split[...] = jnp.concatenate([high, scale - high], axis=0).T.astype(BF16)
    for i, copy in enumerate(copies):
        copy.wait()
        at = slice(i * step, (i + 1) * step)
        for n in range(blocks // 2):
            if n % 4 == 0:
                for b in (2 * n, 2 * n + 1):
                    cols = slice(b * QB, (b + 1) * QB)
                    out[at, cols] = (out[at, cols].astype(F32) * column[at, b : b + 1]).astype(BF16)
            else:
                cols = slice(2 * n * QB, 2 * (n + 1) * QB)
                wide = jnp.dot(split[at, :], spread[:, cols], preferred_element_type=F32)
                out[at, cols] = (out[at, cols].astype(F32) * wide).astype(BF16)


def dequant(code, scale_t):
    rows, width = code.shape
    blocks = scale_t.shape[0]
    step = min(512, rows)
    code = pltpu.with_memory_space_constraint(code, pltpu.HBM)
    scale_t = pltpu.with_memory_space_constraint(scale_t, pltpu.HBM)
    in_hbm = pl.BlockSpec(memory_space=pltpu.HBM)
    return pl.pallas_call(
        functools.partial(dequant_kernel, step),
        in_specs=[in_hbm, in_hbm],
        out_specs=whole(),
        out_shape=VMEM((rows, width), BF16),
        scratch_shapes=[
            pltpu.SemaphoreType.DMA((rows // step,)),
            pltpu.SemaphoreType.DMA,
            VMEM(scale_t.shape, F32),
            VMEM((2 * blocks, width), BF16),
            VMEM((rows, 2 * blocks), BF16),
            VMEM((rows, blocks), F32),
        ],
        compiler_params=pltpu.CompilerParams(vmem_limit_bytes=4 * MIB),
        cost_estimate=pl.CostEstimate(flops=5 * 10**9, bytes_accessed=2 * rows * width, transcendentals=0),
    )(code, scale_t)


def hidden_kernel(parts, groups, span, place, *refs):
    xs, (w_gate, w_up, out, staged) = refs[: groups * parts], refs[groups * parts :]
    part = xs[0].shape[1]
    low, high = span
    block = min(256, high - low)
    at = [pl.ds(pl.multiple_of(lax.rem(place[1] + p, parts) * part, part), part) for p in range(parts)]
    row = 0
    for g in range(groups):
        for p in range(parts):
            x = xs[g * parts + p]
            staged[row : row + x.shape[0], p * part : (p + 1) * part] = x[...]
        row += x.shape[0]
    for n in range((high - low) // block):
        cols = slice(low + n * block, low + (n + 1) * block)
        gate = up = None
        for p in range(parts):
            x = staged[:, p * part : (p + 1) * part]
            g = jnp.dot(x, w_gate[at[p], cols], preferred_element_type=F32)
            u = jnp.dot(x, w_up[at[p], cols], preferred_element_type=F32)
            gate = g if gate is None else gate + g
            up = u if up is None else up + u
        out[:, n * block : (n + 1) * block] = (gate / (1.0 + jnp.exp(-gate)) * up).astype(BF16)


def hidden_of(place, xs, w_gate, w_up, span):
    parts = len(xs[0])
    flat = [x for group in xs for x in group]
    rows = sum(group[0].shape[0] for group in xs)
    width = span[1] - span[0]
    return pl.pallas_call(
        functools.partial(hidden_kernel, parts, len(xs), span),
        in_specs=[scalar()] + [whole()] * (len(flat) + 2),
        out_specs=whole(),
        out_shape=jax.ShapeDtypeStruct((rows, width), BF16),
        scratch_shapes=[VMEM((rows, w_gate.shape[0]), BF16)],
        compiler_params=pltpu.CompilerParams(vmem_limit_bytes=4 * MIB),
        cost_estimate=pl.CostEstimate(
            flops=4 * rows * w_gate.shape[0] * width, bytes_accessed=0, transcendentals=rows * width
        ),
    )(place, *flat, w_gate, w_up)


def down_kernel(count, shift, parts, place, *refs):
    hs, w, outs = refs[:count], refs[count], refs[count + 1 :]
    part = outs[0].shape[1]
    block = min(256, part)
    base = lax.rem(place[1] + shift, parts) * part
    for n in range(part // block):
        at = pl.ds(pl.multiple_of(base + n * block, block), block)
        total, low = None, 0
        for h in hs:
            got = jnp.dot(h[...], w[low : low + h.shape[1], at], preferred_element_type=F32)
            total = got if total is None else total + got
            low += h.shape[1]
        row = 0
        for out in outs:
            size = out.shape[0]
            out[:, n * block : (n + 1) * block] = total[row : row + size, :].astype(out.dtype)
            row += size


def down(place, hs, w, sizes, shift, parts, dtype):
    part = w.shape[1] // parts
    rows = sum(sizes)
    return pl.pallas_call(
        functools.partial(down_kernel, len(hs), shift, parts),
        in_specs=[scalar()] + [whole()] * (len(hs) + 1),
        out_specs=[whole()] * len(sizes),
        out_shape=[jax.ShapeDtypeStruct((size, part), dtype) for size in sizes],
        compiler_params=pltpu.CompilerParams(vmem_limit_bytes=4 * MIB),
        cost_estimate=pl.CostEstimate(flops=2 * rows * w.shape[0] * part, bytes_accessed=0, transcendentals=0),
    )(place, *hs, w)


def join_kernel(*refs):
    *ins, out = refs
    row = 0
    for ref in ins:
        out[row : row + ref.shape[0], :] = ref[...]
        row += ref.shape[0]


def join(xs):
    rows = sum(x.shape[0] for x in xs)
    return pl.pallas_call(
        join_kernel,
        in_specs=[whole()] * len(xs),
        out_specs=whole(),
        out_shape=jax.ShapeDtypeStruct((rows, xs[0].shape[1]), BF16),
        compiler_params=pltpu.CompilerParams(vmem_limit_bytes=2 * MIB),
    )(*xs)


def add_kernel(starts, *refs):
    *ins, out = refs
    rows = out.shape[0]
    total = None
    for start, ref in zip(starts, ins):
        term = ref[start : start + rows, :].astype(F32)
        total = term if total is None else total + term
    out[...] = total.astype(out.dtype)


def add_rows(terms, starts):
    return pl.pallas_call(
        functools.partial(add_kernel, starts),
        in_specs=[whole()] * len(terms),
        out_specs=whole(),
        out_shape=jax.ShapeDtypeStruct((CAP, terms[0].shape[1]), BF16),
        compiler_params=pltpu.CompilerParams(vmem_limit_bytes=1 * MIB),
    )(*terms)


def plan_kernel(place, routes_ref, weight_ref, *refs):
    *picks, weights = refs
    own = place[0]
    routes_t = routes_ref[...]
    count = routes_t.shape[1]
    weights[...] = weight_ref[...].T
    slots = lax.broadcasted_iota(jnp.int32, (CAP, TOP * count), 0)
    both = jnp.concatenate([routes_t[k : k + 1, :] for k in range(TOP)], axis=1)
    for d, pick in enumerate(picks):
        expert = own ^ d
        _, rank = ranks(routes_t, expert)
        wide = jnp.concatenate([rank] * TOP, axis=1).astype(jnp.int32)
        hit = (slots == wide) & (jnp.broadcast_to(both, slots.shape) == expert)
        pick[...] = jnp.where(hit, 1.0, 0.0).T.astype(BF16)


def plan(place, routes_t, weight_t):
    count = routes_t.shape[1]
    *picks, weights = pl.pallas_call(
        plan_kernel,
        in_specs=[scalar()] + [whole()] * 2,
        out_specs=[whole()] * (EXPERTS + 1),
        out_shape=[jax.ShapeDtypeStruct((TOP * count, CAP), BF16)] * EXPERTS
        + [jax.ShapeDtypeStruct((count, TOP), F32)],
        compiler_params=pltpu.CompilerParams(vmem_limit_bytes=4 * MIB),
        name="plan",
    )(place, routes_t, weight_t)
    return picks, weights


def mix_kernel(*refs):
    weights, *refs, out = refs
    picks, pieces = refs[:EXPERTS], refs[EXPERTS:]
    count = out.shape[0]
    gathered = None
    for pick, piece in zip(picks, pieces):
        got = jnp.dot(pick[...], piece[...], preferred_element_type=F32)
        gathered = got if gathered is None else gathered + got
    total = None
    for k in range(TOP):
        term = gathered[k * count : (k + 1) * count, :] * weights[:, k : k + 1]
        total = term if total is None else total + term
    out[...] = total.astype(BF16)


def mix(weights, picks, pieces):
    return pl.pallas_call(
        mix_kernel,
        in_specs=[whole()] * (1 + len(picks) + len(pieces)),
        out_specs=whole(),
        out_shape=jax.ShapeDtypeStruct((weights.shape[0], pieces[0].shape[1]), BF16),
        compiler_params=pltpu.CompilerParams(vmem_limit_bytes=4 * MIB),
        name="mix",
    )(weights, *picks, *pieces)


FAR, NEAR = (3, 2), (1, 0)


def layer(
    members, parts, tokens, routes, route_weight,
    gate_code, gate_scale, up_code, up_scale, down_code, down_scale,
):
    def send(x, where):
        pairs = []
        for e in range(EXPERTS):
            for m in range(members):
                for t in range(parts):
                    e2, m2, t2 = where(e, m, t)
                    pairs.append(((e * members + m) * parts + t, (e2 * members + m2) * parts + t2))
        return lax.ppermute(x, ("ep", "tp"), pairs)

    def to_expert(x, d):
        return x if d == 0 else send(x, lambda e, m, t: (e ^ d, m, t))

    def to_member(x, s):
        return x if s == 0 else send(x, lambda e, m, t: (e, (m + s) % members, t))

    def to_part(x, p):
        return x if p == 0 else send(x, lambda e, m, t: (e, m, (t + p) % parts))

    place = jnp.stack([lax.axis_index("ep") // members, lax.axis_index("tp")]).astype(jnp.int32)
    routes_t, weight_t = routes.T, route_weight.T
    order = FAR + NEAR
    groups = range(members)

    outgoing = pack(place, routes_t, tokens, parts)
    arrived = {d: to_expert(outgoing[d], d) for d in order}
    shared = {(s, d): to_member(arrived[d], s) for d in order for s in groups}

    w_gate = dequant(gate_code, gate_scale.T)
    w_up = dequant(up_code, up_scale.T)
    w_down = dequant(down_code, down_scale.T)

    def rows_of(chunk):
        xs = []
        for s in groups:
            own = join([shared[s, d] for d in chunk])
            xs.append([to_part(own, (parts - p) % parts) for p in range(parts)])
        return xs

    def reduced(chunk, hs):
        sizes = [CAP * len(chunk)] * members
        terms = [[] for _ in groups]
        for p in range(1, parts):
            partial = down(place, hs, w_down, sizes, p, parts, BF16)
            for s in reversed(groups):
                terms[s].append(to_part(partial[s], p))
        own = down(place, hs, w_down, sizes, 0, parts, F32)
        for s in groups:
            terms[s].append(own[s])
        return terms

    def returned(chunk, terms):
        pieces = {}
        for i, d in enumerate(chunk):
            start = i * CAP
            all_terms, starts = list(terms[0]), [start] * len(terms[0])
            for s in range(1, members):
                total = add_rows(terms[s], [start] * len(terms[s]))
                all_terms.append(to_member(total, members - s))
                starts.append(0)
            total = add_rows(all_terms, starts)
            pieces[d] = to_expert(total, d)
        return pieces

    units = w_gate.shape[1]
    far_hidden = hidden_of(place, rows_of(FAR), w_gate, w_up, (0, units))
    far_terms = reduced(FAR, [far_hidden])
    near_rows = rows_of(NEAR)
    half = units // 2
    near_hidden = [
        hidden_of(place, near_rows, w_gate, w_up, (0, half)),
        hidden_of(place, near_rows, w_gate, w_up, (half, units)),
    ]
    pieces = returned(FAR, far_terms)
    near_terms = reduced(NEAR, near_hidden)
    pieces.update(returned(NEAR, near_terms))
    picks, weights = plan(place, routes_t, weight_t)
    return mix(weights, picks, [pieces[d] for d in range(EXPERTS)])


def solution(mesh):
    members = mesh.shape["ep"] // EXPERTS
    parts = mesh.shape["tp"]
    rows = P(("rep", "ep"), None)
    columns = P(None, ("ep", "tp"))
    placed = (rows, rows, rows, columns, columns, columns, columns, P(("ep", "tp"), None), P(("ep", "tp"), None))

    def body(*args):
        return layer(members, parts, *args)

    return jax.shard_map(
        body, mesh=mesh, in_specs=placed, out_specs=P(("rep", "ep"), "tp"), check_vma=False
    )
```

profile of v0, /device:TPU:0, one launch (start us, length us, event | category | flops | bytes accessed | tf_op | source)
XLA Modules:
  0.0 83.9 jit_solution(4391198499397905387)
XLA Ops:
  0.1 0.7 copy-done.2
  0.8 2.3 %pack.1 = (bf16[40,1536]{1,0:T(8,128)(2,1)S(1)}, bf16[40,1536]{1,0:T(8,128)(2,1)S(1)}, bf16[40,1536]{1,0:T(8,128)(2,1)S(1)}, bf16[40,1536]{1,0:T(8,128)(2,1)S(1)}) custom-call(s32[2]{0:T(128)S(1)} %pad_add_fusion.place, s32[2,64]{1,0:T(2,128)S(1)} %bitcast.7, bf16[64,3072]{1,0:T(8,128)(2,1)} %tokens_ref.1), custom_call_target="tpu_custom_call" | custom-call | tf_op jit(solution)/shard_map/pack/pallas_call | solution.py:56
  3.0 5.1 %collective-permute-start.10 = (bf16[40,1536]{1,0:T(8,128)(2,1)S(1)}, bf16[40,1536]{1,0:T(8,128)(2,1)S(1)}, u32[]{:S(2)}, u32[]{:S(2)}) collective-permute-start(bf16[40,1536]{1,0:T(8,128)(2,1)S(1)} %get-tuple-element.33), channel_id=1, source_target_pairs={{0,12},{1,13},{2,14},{3,15},{4,8},{5,9},{6,10},{7,11},{8,4},{9,5},... | collective-permute-start | bytes 368648 | tf_op jit(solution)/shard_map/ppermute | solution.py:314
  8.2 0.6 collective-permute-start
  8.8 1.7 %collective-permute-start.3 = (bf16[40,1536]{1,0:T(8,128)(2,1)S(1)}, bf16[40,1536]{1,0:T(8,128)(2,1)S(1)}, u32[]{:S(2)}, u32[]{:S(2)}) collective-permute-start(bf16[40,1536]{1,0:T(8,128)(2,1)S(1)} %get-tuple-element.28.refs_1_), channel_id=1, source_target_pairs={{0,2},{1,3},{2,0},{3,1},{4,6},{5,7},{6,4},{7,5},{8,10},{9,11},{10,... | collective-permute-start | bytes 368648 | tf_op jit(solution)/shard_map/ppermute | solution.py:314
  10.5 8.2 %shard_map.93.refs_4_ = bf16[3072,2048]{1,0:T(8,128)(2,1)S(1)} custom-call(bf16[3072,2048]{1,0:T(8,128)(2,1)} %code.3, f32[16,3072]{1,0:T(8,128)} %bitcast.10), custom_call_target="tpu_custom_call" | custom-call | flops 5000000000 | bytes 12582912 | tf_op jit(solution)/shard_map/pallas_call | solution.py:113
  18.7 0.4 collective-permute-start.13
  19.1 1.7 %collective-permute-start.14 = (bf16[40,1536]{1,0:T(8,128)(2,1)S(1)}, bf16[40,1536]{1,0:T(8,128)(2,1)S(1)}, u32[]{:S(2)}, u32[]{:S(2)}) collective-permute-start(bf16[40,1536]{1,0:T(8,128)(2,1)S(1)} %collective-permute-done.11.refs_1_), channel_id=1, source_target_pairs={{0,2},{1,3},{2,0},{3,1},{4,6},{5,7},{6,4},{7,5},{8,10},{9,11},{10,... | collective-permute-start | bytes 368648 | tf_op jit(solution)/shard_map/ppermute | solution.py:314
  20.8 8.1 %shard_map.94.refs_5_ = bf16[3072,2048]{1,0:T(8,128)(2,1)S(1)} custom-call(bf16[3072,2048]{1,0:T(8,128)(2,1)} %code.4, f32[16,3072]{1,0:T(8,128)} %bitcast.11), custom_call_target="tpu_custom_call" | custom-call | flops 5000000000 | bytes 12582912 | tf_op jit(solution)/shard_map/pallas_call | solution.py:113
  29.0 0.4 collective-permute-start.2
  29.7 11.4 %shard_map.97.refs_2_.refs_1_ = bf16[2048,3072]{1,0:T(8,128)(2,1)S(1)} custom-call(bf16[2048,3072]{1,0:T(8,128)(2,1)} %code.5, f32[24,2048]{1,0:T(8,128)} %bitcast.12), custom_call_target="tpu_custom_call" | custom-call | flops 5000000000 | bytes 12582912 | tf_op jit(solution)/shard_map/pallas_call | solution.py:113
  41.3 0.5 collective-permute-start.4
  41.8 5.1 %shard_map.106.refs_0_ = bf16[160,2048]{1,0:T(8,128)(2,1)S(1)} custom-call(s32[2]{0:T(128)S(1)} %pad_add_fusion.place, bf16[80,1536]{1,0:T(8,128)(2,1)S(1)} %shard_map.104.refs_0_, bf16[80,1536]{1,0:T(8,128)(2,1)S(1)} %collective-permute-done.12.refs_1_, bf16[80,1536]{1,0:T(8,128)(2,1)S(1)} %shard_map.105.refs_2_, ...), custom_call_target="tpu_custom_call" | custom-call | flops 4026531840 | tf_op jit(solution)/shard_map/pallas_call | solution.py:160
  46.9 1.8 %shard_map.107 = (bf16[80,1536]{1,0:T(8,128)(2,1)S(1)}, bf16[80,1536]{1,0:T(8,128)(2,1)S(1)}) custom-call(s32[2]{0:T(128)S(1)} %pad_add_fusion.place, bf16[160,2048]{1,0:T(8,128)(2,1)S(1)} %shard_map.106.refs_0_, bf16[2048,3072]{1,0:T(8,128)(2,1)S(1)} %shard_map.97.refs_2_.refs_1_), custom_call_target="tpu_custom_call" | custom-call | flops 1006632960 | tf_op jit(solution)/shard_map/pallas_call | solution.py:195
  48.8 4.6 %copy-done.1 = bf16[3072,2048]{1,0:T(8,128)(2,1)S(1)} copy-done((bf16[3072,2048]{1,0:T(8,128)(2,1)S(1)}, bf16[3072,2048]{1,0:T(8,128)(2,1)}, u32[]{:S(2)}) %copy-start.1) | copy-done | bytes 12582936
  53.4 2.8 %shard_map.96.refs_1_ = bf16[160,1024]{1,0:T(8,128)(2,1)S(1)} custom-call(s32[2]{0:T(128)S(1)} %pad_add_fusion.place, bf16[80,1536]{1,0:T(8,128)(2,1)S(1)} %shard_map.91.refs_0_, bf16[80,1536]{1,0:T(8,128)(2,1)S(1)} %collective-permute-done.1.refs_1_, bf16[80,1536]{1,0:T(8,128)(2,1)S(1)} %shard_map.92.refs_2_, ...), custom_call_target="tpu_custom_call" | custom-call | flops 2013265920 | tf_op jit(solution)/shard_map/pallas_call | solution.py:160
  56.2 2.8 %shard_map.95.refs_0_ = bf16[160,1024]{1,0:T(8,128)(2,1)S(1)} custom-call(s32[2]{0:T(128)S(1)} %pad_add_fusion.place, bf16[80,1536]{1,0:T(8,128)(2,1)S(1)} %shard_map.91.refs_0_, bf16[80,1536]{1,0:T(8,128)(2,1)S(1)} %collective-permute-done.1.refs_1_, bf16[80,1536]{1,0:T(8,128)(2,1)S(1)} %shard_map.92.refs_2_, ...), custom_call_target="tpu_custom_call" | custom-call | flops 2013265920 | tf_op jit(solution)/shard_map/pallas_call | solution.py:160
  59.0 1.8 %shard_map.98 = (bf16[80,1536]{1,0:T(8,128)(2,1)S(1)}, bf16[80,1536]{1,0:T(8,128)(2,1)S(1)}) custom-call(s32[2]{0:T(128)S(1)} %pad_add_fusion.place, bf16[160,1024]{1,0:T(8,128)(2,1)S(1)} %shard_map.95.refs_0_, bf16[160,1024]{1,0:T(8,128)(2,1)S(1)} %shard_map.96.refs_1_, bf16[2048,3072]{1,0:T(8,128)(2,1)S(1)} %shard_map.97.refs_2_.refs_1_), custom_call_target="tpu_custom_call" | custom-call | flops 1006632960 | tf_op jit(solution)/shard_map/pallas_call | solution.py:195
  60.8 0.5 collective-permute-start.6
  61.4 0.4 collective-permute-start.5
  61.8 1.8 %shard_map.108 = (f32[80,1536]{1,0:T(8,128)S(1)}, f32[80,1536]{1,0:T(8,128)S(1)}) custom-call(s32[2]{0:T(128)S(1)} %pad_add_fusion.place, bf16[160,2048]{1,0:T(8,128)(2,1)S(1)} %shard_map.106.refs_0_, bf16[2048,3072]{1,0:T(8,128)(2,1)S(1)} %shard_map.97.refs_2_.refs_1_), custom_call_target="tpu_custom_call" | custom-call | flops 1006632960 | tf_op jit(solution)/shard_map/pallas_call | solution.py:195
  63.7 0.3 collective-permute-start.20
  64.0 1.8 %shard_map.99 = (f32[80,1536]{1,0:T(8,128)S(1)}, f32[80,1536]{1,0:T(8,128)S(1)}) custom-call(s32[2]{0:T(128)S(1)} %pad_add_fusion.place, bf16[160,1024]{1,0:T(8,128)(2,1)S(1)} %shard_map.95.refs_0_, bf16[160,1024]{1,0:T(8,128)(2,1)S(1)} %shard_map.96.refs_1_, bf16[2048,3072]{1,0:T(8,128)(2,1)S(1)} %shard_map.97.refs_2_.refs_1_), custom_call_target="tpu_custom_call" | custom-call | flops 1006632960 | tf_op jit(solution)/shard_map/pallas_call | solution.py:195
  65.8 1.9 %collective-permute-start.18 = (bf16[40,1536]{1,0:T(8,128)(2,1)S(1)}, bf16[40,1536]{1,0:T(8,128)(2,1)S(1)}, u32[]{:S(2)}, u32[]{:S(2)}) collective-permute-start(bf16[40,1536]{1,0:T(8,128)(2,1)S(1)} %shard_map.109), channel_id=1, source_target_pairs={{0,2},{1,3},{2,0},{3,1},{4,6},{5,7},{6,4},{7,5},{8,10},{9,11},{10,... | collective-permute-start | bytes 368648 | tf_op jit(solution)/shard_map/ppermute | solution.py:314
  68.0 1.9 %collective-permute-start.7 = (bf16[40,1536]{1,0:T(8,128)(2,1)S(1)}, bf16[40,1536]{1,0:T(8,128)(2,1)S(1)}, u32[]{:S(2)}, u32[]{:S(2)}) collective-permute-start(bf16[40,1536]{1,0:T(8,128)(2,1)S(1)} %shard_map.100), channel_id=1, source_target_pairs={{0,2},{1,3},{2,0},{3,1},{4,6},{5,7},{6,4},{7,5},{8,10},{9,11},{10,... | collective-permute-start | bytes 368648 | tf_op jit(solution)/shard_map/ppermute | solution.py:314
  69.9 3.6 %collective-permute-start.21 = (bf16[40,1536]{1,0:T(8,128)(2,1)S(1)}, bf16[40,1536]{1,0:T(8,128)(2,1)S(1)}, u32[]{:S(2)}, u32[]{:S(2)}) collective-permute-start(bf16[40,1536]{1,0:T(8,128)(2,1)S(1)} %shard_map.112), channel_id=1, source_target_pairs={{0,12},{1,13},{2,14},{3,15},{4,8},{5,9},{6,10},{7,11},{8,4},{9,5},... | collective-permute-start | bytes 368648 | tf_op jit(solution)/shard_map/ppermute | solution.py:314
  73.6 1.0 %collective-permute-start.19 = (bf16[40,1536]{1,0:T(8,128)(2,1)S(1)}, bf16[40,1536]{1,0:T(8,128)(2,1)S(1)}, u32[]{:S(2)}, u32[]{:S(2)}) collective-permute-start(bf16[40,1536]{1,0:T(8,128)(2,1)S(1)} %shard_map.110), channel_id=1, source_target_pairs={{0,8},{1,9},{2,10},{3,11},{4,12},{5,13},{6,14},{7,15},{8,0},{9,1},... | collective-permute-start | bytes 368648 | tf_op jit(solution)/shard_map/ppermute | solution.py:314
  74.5 0.5 collective-permute-done.8.refs_2_
  75.1 1.5 %collective-permute-start.9 = (bf16[40,1536]{1,0:T(8,128)(2,1)S(1)}, bf16[40,1536]{1,0:T(8,128)(2,1)S(1)}, u32[]{:S(2)}, u32[]{:S(2)}) collective-permute-start(bf16[40,1536]{1,0:T(8,128)(2,1)S(1)} %shard_map.103), channel_id=1, source_target_pairs={{0,4},{1,5},{2,6},{3,7},{4,0},{5,1},{6,2},{7,3},{8,12},{9,13},{10,... | collective-permute-start | bytes 368648 | tf_op jit(solution)/shard_map/ppermute | solution.py:314
  76.6 1.0 %plan.1 = (bf16[128,40]{1,0:T(8,128)(2,1)S(1)}, bf16[128,40]{1,0:T(8,128)(2,1)S(1)}, bf16[128,40]{1,0:T(8,128)(2,1)S(1)}, bf16[128,40]{1,0:T(8,128)(2,1)S(1)}, f32[64,2]{1,0:T(8,128)S(1)}) custom-call(s32[2]{0:T(128)S(1)} %pad_add_fusion.place, s32[2,64]{1,0:T(2,128)S(1)} %bitcast.8, f32[2,64]{1,0:T(2,128)S(1)} %bitcast.9), custom_call_target="tpu_custom_call" | custom-call | tf_op jit(solution)/shard_map/plan/pallas_call | solution.py:262
  77.7 5.0 %collective-permute-done.19.refs_7_ = bf16[40,1536]{1,0:T(8,128)(2,1)S(1)} collective-permute-done((bf16[40,1536]{1,0:T(8,128)(2,1)S(1)}, bf16[40,1536]{1,0:T(8,128)(2,1)S(1)}, u32[]{:S(2)}, u32[]{:S(2)}) %collective-permute-start.19) | collective-permute-done | bytes 122912 | tf_op jit(solution)/shard_map/ppermute | solution.py:314
  82.7 1.2 %mix.1 = bf16[64,1536]{1,0:T(8,128)(2,1)} custom-call(f32[64,2]{1,0:T(8,128)S(1)} %get-tuple-element.22.refs_0_, bf16[128,40]{1,0:T(8,128)(2,1)S(1)} %get-tuple-element.23.refs_1_, bf16[128,40]{1,0:T(8,128)(2,1)S(1)} %get-tuple-element.24.refs_2_, bf16[128,40]{1,0:T(8,128)(2,1)S(1)} %get-tuple-element.25.refs_3_, ...), custom_call_target="tpu_custom_call" | custom-call | tf_op jit(solution)/shard_map/mix/pallas_call | solution.py:290
  (46 shorter events, 1.3 us)
Async XLA Ops:
  0.1 0.7 copy-start.2
  3.0 15.6 %collective-permute-start.10 = (bf16[40,1536]{1,0:T(8,128)(2,1)S(1)}, bf16[40,1536]{1,0:T(8,128)(2,1)S(1)}, u32[]{:S(2)}, u32[]{:S(2)}) collective-permute-start(bf16[40,1536]{1,0:T(8,128)(2,1)S(1)} %get-tuple-element.33), channel_id=1, source_target_pairs={{0,12},{1,13},{2,14},{3,15},{4,8},{5,9},{6,10},{7,11},{8,4},{9,5},... | collective-permute-start | bytes 368648 | tf_op jit(solution)/shard_map/ppermute | solution.py:314
  8.2 10.9 %collective-permute-start.11 = (bf16[40,1536]{1,0:T(8,128)(2,1)S(1)}, bf16[40,1536]{1,0:T(8,128)(2,1)S(1)}, u32[]{:S(2)}, u32[]{:S(2)}) collective-permute-start(bf16[40,1536]{1,0:T(8,128)(2,1)S(1)} %get-tuple-element.34), channel_id=1, source_target_pairs={{0,8},{1,9},{2,10},{3,11},{4,12},{5,13},{6,14},{7,15},{8,0},{9,1},... | collective-permute-start | bytes 368648 | tf_op jit(solution)/shard_map/ppermute | solution.py:314
  8.2 20.8 %collective-permute-start = (bf16[40,1536]{1,0:T(8,128)(2,1)S(1)}, bf16[40,1536]{1,0:T(8,128)(2,1)S(1)}, u32[]{:S(2)}, u32[]{:S(2)}) collective-permute-start(bf16[40,1536]{1,0:T(8,128)(2,1)S(1)} %get-tuple-element.27), channel_id=1, source_target_pairs={{0,4},{1,5},{2,6},{3,7},{4,0},{5,1},{6,2},{7,3},{8,12},{9,13},{10,... | collective-permute-start | bytes 368648 | tf_op jit(solution)/shard_map/ppermute | solution.py:314
  8.8 32.4 %collective-permute-start.3 = (bf16[40,1536]{1,0:T(8,128)(2,1)S(1)}, bf16[40,1536]{1,0:T(8,128)(2,1)S(1)}, u32[]{:S(2)}, u32[]{:S(2)}) collective-permute-start(bf16[40,1536]{1,0:T(8,128)(2,1)S(1)} %get-tuple-element.28.refs_1_), channel_id=1, source_target_pairs={{0,2},{1,3},{2,0},{3,1},{4,6},{5,7},{6,4},{7,5},{8,10},{9,11},{10,... | collective-permute-start | bytes 368648 | tf_op jit(solution)/shard_map/ppermute | solution.py:314
  18.7 10.8 %collective-permute-start.13 = (bf16[40,1536]{1,0:T(8,128)(2,1)S(1)}, bf16[40,1536]{1,0:T(8,128)(2,1)S(1)}, u32[]{:S(2)}, u32[]{:S(2)}) collective-permute-start(bf16[40,1536]{1,0:T(8,128)(2,1)S(1)} %collective-permute-done.10.refs_0_), channel_id=1, source_target_pairs={{0,2},{1,3},{2,0},{3,1},{4,6},{5,7},{6,4},{7,5},{8,10},{9,11},{10,... | collective-permute-start | bytes 368648 | tf_op jit(solution)/shard_map/ppermute | solution.py:314
  19.1 10.4 %collective-permute-start.14 = (bf16[40,1536]{1,0:T(8,128)(2,1)S(1)}, bf16[40,1536]{1,0:T(8,128)(2,1)S(1)}, u32[]{:S(2)}, u32[]{:S(2)}) collective-permute-start(bf16[40,1536]{1,0:T(8,128)(2,1)S(1)} %collective-permute-done.11.refs_1_), channel_id=1, source_target_pairs={{0,2},{1,3},{2,0},{3,1},{4,6},{5,7},{6,4},{7,5},{8,10},{9,11},{10,... | collective-permute-start | bytes 368648 | tf_op jit(solution)/shard_map/ppermute | solution.py:314
  28.9 12.9 %copy-start = (bf16[3072,2048]{1,0:T(8,128)(2,1)}, bf16[3072,2048]{1,0:T(8,128)(2,1)S(1)}, u32[]{:S(2)}) copy-start(bf16[3072,2048]{1,0:T(8,128)(2,1)S(1)} %shard_map.94.refs_5_) | copy-start | bytes 37748740
  28.9 12.9 %collective-permute-start.12 = (bf16[80,1536]{1,0:T(8,128)(2,1)S(1)}, bf16[80,1536]{1,0:T(8,128)(2,1)S(1)}, u32[]{:S(2)}, u32[]{:S(2)}) collective-permute-start(bf16[80,1536]{1,0:T(8,128)(2,1)S(1)} %shard_map.104.refs_0_), channel_id=1, source_target_pairs={{0,1},{1,0},{2,3},{3,2},{4,5},{5,4},{6,7},{7,6},{8,9},{9,8},{10,11... | collective-permute-start | bytes 737288 | tf_op jit(solution)/shard_map/ppermute | solution.py:314
  29.0 12.2 %collective-permute-start.2 = (bf16[40,1536]{1,0:T(8,128)(2,1)S(1)}, bf16[40,1536]{1,0:T(8,128)(2,1)S(1)}, u32[]{:S(2)}, u32[]{:S(2)}) collective-permute-start(bf16[40,1536]{1,0:T(8,128)(2,1)S(1)} %collective-permute-done.refs_0_), channel_id=1, source_target_pairs={{0,2},{1,3},{2,0},{3,1},{4,6},{5,7},{6,4},{7,5},{8,10},{9,11},{10,... | collective-permute-start | bytes 368648 | tf_op jit(solution)/shard_map/ppermute | solution.py:314
  29.5 12.3 %collective-permute-start.15 = (bf16[80,1536]{1,0:T(8,128)(2,1)S(1)}, bf16[80,1536]{1,0:T(8,128)(2,1)S(1)}, u32[]{:S(2)}, u32[]{:S(2)}) collective-permute-start(bf16[80,1536]{1,0:T(8,128)(2,1)S(1)} %shard_map.105.refs_2_), channel_id=1, source_target_pairs={{0,1},{1,0},{2,3},{3,2},{4,5},{5,4},{6,7},{7,6},{8,9},{9,8},{10,11... | collective-permute-start | bytes 737288 | tf_op jit(solution)/shard_map/ppermute | solution.py:314
  41.1 7.6 %collective-permute-start.1 = (bf16[80,1536]{1,0:T(8,128)(2,1)S(1)}, bf16[80,1536]{1,0:T(8,128)(2,1)S(1)}, u32[]{:S(2)}, u32[]{:S(2)}) collective-permute-start(bf16[80,1536]{1,0:T(8,128)(2,1)S(1)} %shard_map.91.refs_0_), channel_id=1, source_target_pairs={{0,1},{1,0},{2,3},{3,2},{4,5},{5,4},{6,7},{7,6},{8,9},{9,8},{10,11... | collective-permute-start | bytes 737288 | tf_op jit(solution)/shard_map/ppermute | solution.py:314
  41.3 7.5 %collective-permute-start.4 = (bf16[80,1536]{1,0:T(8,128)(2,1)S(1)}, bf16[80,1536]{1,0:T(8,128)(2,1)S(1)}, u32[]{:S(2)}, u32[]{:S(2)}) collective-permute-start(bf16[80,1536]{1,0:T(8,128)(2,1)S(1)} %shard_map.92.refs_2_), channel_id=1, source_target_pairs={{0,1},{1,0},{2,3},{3,2},{4,5},{5,4},{6,7},{7,6},{8,9},{9,8},{10,11... | collective-permute-start | bytes 737288 | tf_op jit(solution)/shard_map/ppermute | solution.py:314
  48.7 14.9 %collective-permute-start.17 = (bf16[80,1536]{1,0:T(8,128)(2,1)S(1)}, bf16[80,1536]{1,0:T(8,128)(2,1)S(1)}, u32[]{:S(2)}, u32[]{:S(2)}) collective-permute-start(bf16[80,1536]{1,0:T(8,128)(2,1)S(1)} %get-tuple-element.37), channel_id=1, source_target_pairs={{0,1},{1,0},{2,3},{3,2},{4,5},{5,4},{6,7},{7,6},{8,9},{9,8},{10,11... | collective-permute-start | bytes 737288 | tf_op jit(solution)/shard_map/ppermute | solution.py:314
  48.8 4.6 %copy-start.1 = (bf16[3072,2048]{1,0:T(8,128)(2,1)S(1)}, bf16[3072,2048]{1,0:T(8,128)(2,1)}, u32[]{:S(2)}) copy-start(bf16[3072,2048]{1,0:T(8,128)(2,1)} %copy-done) | copy-start | bytes 37748740
  60.8 6.9 %collective-permute-start.6 = (bf16[80,1536]{1,0:T(8,128)(2,1)S(1)}, bf16[80,1536]{1,0:T(8,128)(2,1)S(1)}, u32[]{:S(2)}, u32[]{:S(2)}) collective-permute-start(bf16[80,1536]{1,0:T(8,128)(2,1)S(1)} %get-tuple-element.31), channel_id=1, source_target_pairs={{0,1},{1,0},{2,3},{3,2},{4,5},{5,4},{6,7},{7,6},{8,9},{9,8},{10,11... | collective-permute-start | bytes 737288 | tf_op jit(solution)/shard_map/ppermute | solution.py:314
  61.3 6.7 %collective-permute-start.16 = (bf16[80,1536]{1,0:T(8,128)(2,1)S(1)}, bf16[80,1536]{1,0:T(8,128)(2,1)S(1)}, u32[]{:S(2)}, u32[]{:S(2)}) collective-permute-start(bf16[80,1536]{1,0:T(8,128)(2,1)S(1)} %get-tuple-element.35), channel_id=1, source_target_pairs={{0,1},{1,0},{2,3},{3,2},{4,5},{5,4},{6,7},{7,6},{8,9},{9,8},{10,11... | collective-permute-start | bytes 737288 | tf_op jit(solution)/shard_map/ppermute | solution.py:314
  61.4 13.2 %collective-permute-start.5 = (bf16[80,1536]{1,0:T(8,128)(2,1)S(1)}, bf16[80,1536]{1,0:T(8,128)(2,1)S(1)}, u32[]{:S(2)}, u32[]{:S(2)}) collective-permute-start(bf16[80,1536]{1,0:T(8,128)(2,1)S(1)} %get-tuple-element.29), channel_id=1, source_target_pairs={{0,1},{1,0},{2,3},{3,2},{4,5},{5,4},{6,7},{7,6},{8,9},{9,8},{10,11... | collective-permute-start | bytes 737288 | tf_op jit(solution)/shard_map/ppermute | solution.py:314
  63.6 13.0 %copy-start.3 = (f32[64,2]{0,1:T(2,128)S(1)}, f32[64,2]{0,1:T(2,128)}, u32[]{:S(2)}) copy-start(f32[64,2]{0,1:T(2,128)} %param.11) | copy-start | bytes 1540
  63.7 6.2 %collective-permute-start.20 = (bf16[40,1536]{1,0:T(8,128)(2,1)S(1)}, bf16[40,1536]{1,0:T(8,128)(2,1)S(1)}, u32[]{:S(2)}, u32[]{:S(2)}) collective-permute-start(bf16[40,1536]{1,0:T(8,128)(2,1)S(1)} %shard_map.111), channel_id=1, source_target_pairs={{0,2},{1,3},{2,0},{3,1},{4,6},{5,7},{6,4},{7,5},{8,10},{9,11},{10,... | collective-permute-start | bytes 368648 | tf_op jit(solution)/shard_map/ppermute | solution.py:314
  65.8 7.8 %collective-permute-start.18 = (bf16[40,1536]{1,0:T(8,128)(2,1)S(1)}, bf16[40,1536]{1,0:T(8,128)(2,1)S(1)}, u32[]{:S(2)}, u32[]{:S(2)}) collective-permute-start(bf16[40,1536]{1,0:T(8,128)(2,1)S(1)} %shard_map.109), channel_id=1, source_target_pairs={{0,2},{1,3},{2,0},{3,1},{4,6},{5,7},{6,4},{7,5},{8,10},{9,11},{10,... | collective-permute-start | bytes 368648 | tf_op jit(solution)/shard_map/ppermute | solution.py:314
  67.7 7.4 %collective-permute-start.8 = (bf16[40,1536]{1,0:T(8,128)(2,1)S(1)}, bf16[40,1536]{1,0:T(8,128)(2,1)S(1)}, u32[]{:S(2)}, u32[]{:S(2)}) collective-permute-start(bf16[40,1536]{1,0:T(8,128)(2,1)S(1)} %shard_map.102), channel_id=1, source_target_pairs={{0,2},{1,3},{2,0},{3,1},{4,6},{5,7},{6,4},{7,5},{8,10},{9,11},{10,... | collective-permute-start | bytes 368648 | tf_op jit(solution)/shard_map/ppermute | solution.py:314
  68.0 9.6 %collective-permute-start.7 = (bf16[40,1536]{1,0:T(8,128)(2,1)S(1)}, bf16[40,1536]{1,0:T(8,128)(2,1)S(1)}, u32[]{:S(2)}, u32[]{:S(2)}) collective-permute-start(bf16[40,1536]{1,0:T(8,128)(2,1)S(1)} %shard_map.100), channel_id=1, source_target_pairs={{0,2},{1,3},{2,0},{3,1},{4,6},{5,7},{6,4},{7,5},{8,10},{9,11},{10,... | collective-permute-start | bytes 368648 | tf_op jit(solution)/shard_map/ppermute | solution.py:314
  69.9 7.8 %collective-permute-start.21 = (bf16[40,1536]{1,0:T(8,128)(2,1)S(1)}, bf16[40,1536]{1,0:T(8,128)(2,1)S(1)}, u32[]{:S(2)}, u32[]{:S(2)}) collective-permute-start(bf16[40,1536]{1,0:T(8,128)(2,1)S(1)} %shard_map.112), channel_id=1, source_target_pairs={{0,12},{1,13},{2,14},{3,15},{4,8},{5,9},{6,10},{7,11},{8,4},{9,5},... | collective-permute-start | bytes 368648 | tf_op jit(solution)/shard_map/ppermute | solution.py:314
  73.6 9.1 %collective-permute-start.19 = (bf16[40,1536]{1,0:T(8,128)(2,1)S(1)}, bf16[40,1536]{1,0:T(8,128)(2,1)S(1)}, u32[]{:S(2)}, u32[]{:S(2)}) collective-permute-start(bf16[40,1536]{1,0:T(8,128)(2,1)S(1)} %shard_map.110), channel_id=1, source_target_pairs={{0,8},{1,9},{2,10},{3,11},{4,12},{5,13},{6,14},{7,15},{8,0},{9,1},... | collective-permute-start | bytes 368648 | tf_op jit(solution)/shard_map/ppermute | solution.py:314
  75.1 7.6 %collective-permute-start.9 = (bf16[40,1536]{1,0:T(8,128)(2,1)S(1)}, bf16[40,1536]{1,0:T(8,128)(2,1)S(1)}, u32[]{:S(2)}, u32[]{:S(2)}) collective-permute-start(bf16[40,1536]{1,0:T(8,128)(2,1)S(1)} %shard_map.103), channel_id=1, source_target_pairs={{0,4},{1,5},{2,6},{3,7},{4,0},{5,1},{6,2},{7,3},{8,12},{9,13},{10,... | collective-permute-start | bytes 368648 | tf_op jit(solution)/shard_map/ppermute | solution.py:314
where the time goes:
time: 84.1 us; the launch traced here: 83.9 us
  Pallas kernels  50.3 us (60%)
  starting transfers between devices  22.4 us (27%)
  waiting for transfers between devices  5.59 us (7%)
  local copies, waits for them, and re-layouts  5.26 us (6%)
    pallas_call x3, Pallas kernels, dequant(): pl.pallas_call(functools.partial(dequant_kernel, step), in_specs=[in_hbm,...  27.7 us
    ppermute x22, starting transfers between devices, send(): return lax.ppermute(x, ('ep', 'tp'), pairs)  22.4 us
    pallas_call x3, Pallas kernels, hidden_of(): pl.pallas_call(functools.partial(hidden_kernel, parts, len(xs), span), in...  10.7 us
    pallas_call x4, Pallas kernels, down(): pl.pallas_call(functools.partial(down_kernel, len(hs), shift, parts), in_...  7.12 us
    ppermute x22, waiting for transfers between devices, send(): return lax.ppermute(x, ('ep', 'tp'), pairs)  5.59 us
    unnamed x8, local copies, waits for them, and re-layouts  5.26 us
    pallas_call x1, Pallas kernels, pack(): pl.pallas_call(pack_kernel, grid_spec=pltpu.PrefetchScalarGridSpec(num_sc...  2.27 us
  transfers between devices with their start and end apart: 22, of which 3 were waited for; matrix products, arithmetic and copies ran while one was open for 0% of the time, Pallas kernels for 56%

commit v1 on v0

--- a/solution.py
+++ b/solution.py
@@ -15,6 +15,7 @@
 BF16 = jnp.bfloat16
 VMEM = pltpu.VMEM
 MIB = 2**20
+LANES = 128
 
 
 def whole():
@@ -65,65 +66,67 @@
             out_specs=[pl.BlockSpec((CAP, part), lambda i, place: (0, 0))] * EXPERTS,
         ),
         out_shape=[jax.ShapeDtypeStruct((CAP, part), BF16)] * EXPERTS,
-        compiler_params=pltpu.CompilerParams(vmem_limit_bytes=4 * MIB),
+        compiler_params=pltpu.CompilerParams(vmem_limit_bytes=1 * MIB),
+        cost_estimate=pl.CostEstimate(flops=6 * 10**9, bytes_accessed=0, transcendentals=0),
         name="pack",
     )(place, routes_t, tokens)
 
 
-def dequant_kernel(step, code, scale_hbm, out, sems, scale_sem, scale_ref, spread, split, column):
+def dequant_kernel(step, ahead, code, scale_ref, out, spread, split, column, sems=None):
     rows, _ = out.shape
     blocks = scale_ref.shape[0]
-    scale_copy = pltpu.make_async_copy(scale_hbm, scale_ref, scale_sem)
-    scale_copy.start()
+    pieces = [pl.ds(i * step, step) for i in range(rows // step)]
     copies = []
-    for i in range(rows // step):
-        at = pl.ds(i * step, step)
-        copies.append(pltpu.make_async_copy(code.at[at], out.at[at], sems.at[i]))
-    for copy in copies:
+    if ahead:
+        copies = [pltpu.make_async_copy(code.at[at], out.at[at], sems.at[i]) for i, at in enumerate(pieces)]
+        code = out
+    for copy in copies[:ahead]:
         copy.start()
     row = lax.broadcasted_iota(jnp.int32, spread.shape, 0)
     col = lax.broadcasted_iota(jnp.int32, spread.shape, 1)
     spread[...] = jnp.where(lax.rem(row, blocks) == lax.div(col, QB), 1.0, 0.0).astype(BF16)
-    scale_copy.wait()
     scale = scale_ref[...]
     high = scale.astype(BF16).astype(F32)
     column[...] = scale.T
     split[...] = jnp.concatenate([high, scale - high], axis=0).T.astype(BF16)
-    for i, copy in enumerate(copies):
-        copy.wait()
+    for i in range(rows // step):
+        if ahead:
+            copies[i].wait()
+            if i + ahead < len(copies):
+                copies[i + ahead].start()
         at = slice(i * step, (i + 1) * step)
         for n in range(blocks // 2):
             if n % 4 == 0:
                 for b in (2 * n, 2 * n + 1):
                     cols = slice(b * QB, (b + 1) * QB)
-                    out[at, cols] = (out[at, cols].astype(F32) * column[at, b : b + 1]).astype(BF16)
+                    out[at, cols] = (code[at, cols].astype(F32) * column[at, b : b + 1]).astype(BF16)
             else:
                 cols = slice(2 * n * QB, 2 * (n + 1) * QB)
                 wide = jnp.dot(split[at, :], spread[:, cols], preferred_element_type=F32)
-                out[at, cols] = (out[at, cols].astype(F32) * wide).astype(BF16)
-
-
-def dequant(code, scale_t):
+                out[at, cols] = (code[at, cols].astype(F32) * wide).astype(BF16)
+
+
+def dequant(code, scale_t, ahead):
     rows, width = code.shape
     blocks = scale_t.shape[0]
     step = min(512, rows)
-    code = pltpu.with_memory_space_constraint(code, pltpu.HBM)
-    scale_t = pltpu.with_memory_space_constraint(scale_t, pltpu.HBM)
-    in_hbm = pl.BlockSpec(memory_space=pltpu.HBM)
-    return pl.pallas_call(
-        functools.partial(dequant_kernel, step),
-        in_specs=[in_hbm, in_hbm],
+    first, sems = whole(), []
+    if ahead:
+        code = pltpu.with_memory_space_constraint(code, pltpu.HBM)
+        first = pl.BlockSpec(memory_space=pltpu.HBM)
+        sems = [pltpu.SemaphoreType.DMA((rows // step,))]
+    return pl.pallas_call(
+        functools.partial(dequant_kernel, step, ahead),
+        in_specs=[first, whole()],
         out_specs=whole(),
         out_shape=VMEM((rows, width), BF16),
         scratch_shapes=[
-            pltpu.SemaphoreType.DMA((rows // step,)),
-            pltpu.SemaphoreType.DMA,
-            VMEM(scale_t.shape, F32),
             VMEM((2 * blocks, width), BF16),
             VMEM((rows, 2 * blocks), BF16),
             VMEM((rows, blocks), F32),
+            *sems,
         ],
-        compiler_params=pltpu.CompilerParams(vmem_limit_bytes=4 * MIB),
+        compiler_params=pltpu.CompilerParams(vmem_limit_bytes=MIB // 2 + 6 * LANES * rows),
         cost_estimate=pl.CostEstimate(flops=5 * 10**9, bytes_accessed=2 * rows * width, transcendentals=0),
     )(code, scale_t)
 
@@ -156,14 +159,14 @@
     parts = len(xs[0])
     flat = [x for group in xs for x in group]
     rows = sum(group[0].shape[0] for group in xs)
-    width = span[1] - span[0]
+    depth, width = w_gate.shape[0], span[1] - span[0]
     return pl.pallas_call(
         functools.partial(hidden_kernel, parts, len(xs), span),
         in_specs=[scalar()] + [whole()] * (len(flat) + 2),
         out_specs=whole(),
         out_shape=jax.ShapeDtypeStruct((rows, width), BF16),
         scratch_shapes=[VMEM((rows, w_gate.shape[0]), BF16)],
-        compiler_params=pltpu.CompilerParams(vmem_limit_bytes=4 * MIB),
+        compiler_params=pltpu.CompilerParams(vmem_limit_bytes=2 * MIB + 2 * rows * depth + MIB // 8),
         cost_estimate=pl.CostEstimate(
             flops=4 * rows * w_gate.shape[0] * width, bytes_accessed=0, transcendentals=rows * width
         ),
@@ -197,7 +200,7 @@
         in_specs=[scalar()] + [whole()] * (len(hs) + 1),
         out_specs=[whole()] * len(sizes),
         out_shape=[jax.ShapeDtypeStruct((size, part), dtype) for size in sizes],
-        compiler_params=pltpu.CompilerParams(vmem_limit_bytes=4 * MIB),
+        compiler_params=pltpu.CompilerParams(vmem_limit_bytes=1 * MIB),
         cost_estimate=pl.CostEstimate(flops=2 * rows * w.shape[0] * part, bytes_accessed=0, transcendentals=0),
     )(place, *hs, w)
 
@@ -217,26 +220,26 @@
         in_specs=[whole()] * len(xs),
         out_specs=whole(),
         out_shape=jax.ShapeDtypeStruct((rows, xs[0].shape[1]), BF16),
-        compiler_params=pltpu.CompilerParams(vmem_limit_bytes=2 * MIB),
+        compiler_params=pltpu.CompilerParams(vmem_limit_bytes=1 * MIB),
     )(*xs)
 
 
-def add_kernel(starts, *refs):
-    *ins, out = refs
-    rows = out.shape[0]
-    total = None
-    for start, ref in zip(starts, ins):
-        term = ref[start : start + rows, :].astype(F32)
-        total = term if total is None else total + term
-    out[...] = total.astype(out.dtype)
+def add_kernel(count, starts, *refs):
+    ins, outs = refs[:count], refs[count:]
+    for start, out in zip(starts, outs):
+        total = None
+        for at, ref in zip(start, ins):
+            term = ref[at : at + CAP, :].astype(F32)
+            total = term if total is None else total + term
+        out[...] = total.astype(out.dtype)
 
 
 def add_rows(terms, starts):
     return pl.pallas_call(
-        functools.partial(add_kernel, starts),
+        functools.partial(add_kernel, len(terms), starts),
         in_specs=[whole()] * len(terms),
-        out_specs=whole(),
-        out_shape=jax.ShapeDtypeStruct((CAP, terms[0].shape[1]), BF16),
+        out_specs=[whole()] * len(starts),
+        out_shape=[jax.ShapeDtypeStruct((CAP, terms[0].shape[1]), BF16)] * len(starts),
         compiler_params=pltpu.CompilerParams(vmem_limit_bytes=1 * MIB),
     )(*terms)
 
@@ -271,13 +274,13 @@
     return picks, weights
 
 
-def mix_kernel(*refs):
+def mix_kernel(owners, *refs):
     weights, *refs, out = refs
     picks, pieces = refs[:EXPERTS], refs[EXPERTS:]
     count = out.shape[0]
     gathered = None
-    for pick, piece in zip(picks, pieces):
-        got = jnp.dot(pick[...], piece[...], preferred_element_type=F32)
+    for d, piece in zip(owners, pieces):
+        got = jnp.dot(picks[d][...], piece[...], preferred_element_type=F32)
         gathered = got if gathered is None else gathered + got
     total = None
     for k in range(TOP):
@@ -287,12 +290,14 @@
 
 
 def mix(weights, picks, pieces):
-    return pl.pallas_call(
-        mix_kernel,
+    owners = [d for d in range(EXPERTS) for _ in pieces[d]]
+    pieces = [x for d in range(EXPERTS) for x in pieces[d]]
+    return pl.pallas_call(
+        functools.partial(mix_kernel, owners),
         in_specs=[whole()] * (1 + len(picks) + len(pieces)),
         out_specs=whole(),
         out_shape=jax.ShapeDtypeStruct((weights.shape[0], pieces[0].shape[1]), BF16),
-        compiler_params=pltpu.CompilerParams(vmem_limit_bytes=4 * MIB),
+        compiler_params=pltpu.CompilerParams(vmem_limit_bytes=2 * MIB),
         name="mix",
     )(weights, *picks, *pieces)
 
@@ -329,58 +334,58 @@
 
     outgoing = pack(place, routes_t, tokens, parts)
     arrived = {d: to_expert(outgoing[d], d) for d in order}
-    shared = {(s, d): to_member(arrived[d], s) for d in order for s in groups}
-
-    w_gate = dequant(gate_code, gate_scale.T)
-    w_up = dequant(up_code, up_scale.T)
-    w_down = dequant(down_code, down_scale.T)
+
+    w_gate = dequant(gate_code, gate_scale.T, 0)
+    w_up = dequant(up_code, up_scale.T, 0)
+    w_down = dequant(down_code, down_scale.T, 3)
 
     def rows_of(chunk):
+        joined = join([arrived[d] for d in chunk])
         xs = []
         for s in groups:
-            own = join([shared[s, d] for d in chunk])
+            own = to_member(joined, s)
             xs.append([to_part(own, (parts - p) % parts) for p in range(parts)])
         return xs
 
-    def reduced(chunk, hs):
-        sizes = [CAP * len(chunk)] * members
-        terms = [[] for _ in groups]
+    def reduced(hs, sizes):
+        terms = [[] for _ in sizes]
         for p in range(1, parts):
             partial = down(place, hs, w_down, sizes, p, parts, BF16)
-            for s in reversed(groups):
-                terms[s].append(to_part(partial[s], p))
+            for k in reversed(range(len(sizes))):
+                terms[k].append(to_part(partial[k], p))
         own = down(place, hs, w_down, sizes, 0, parts, F32)
-        for s in groups:
-            terms[s].append(own[s])
+        for k in range(len(sizes)):
+            terms[k].append(own[k])
         return terms
-
-    def returned(chunk, terms):
-        pieces = {}
-        for i, d in enumerate(chunk):
-            start = i * CAP
-            all_terms, starts = list(terms[0]), [start] * len(terms[0])
-            for s in range(1, members):
-                total = add_rows(terms[s], [start] * len(terms[s]))
-                all_terms.append(to_member(total, members - s))
-                starts.append(0)
-            total = add_rows(all_terms, starts)
-            pieces[d] = to_expert(total, d)
-        return pieces
 
     units = w_gate.shape[1]
     far_hidden = hidden_of(place, rows_of(FAR), w_gate, w_up, (0, units))
-    far_terms = reduced(FAR, [far_hidden])
+    far_terms = reduced([far_hidden], [CAP * len(FAR)] * members)
     near_rows = rows_of(NEAR)
     half = units // 2
     near_hidden = [
-        hidden_of(place, near_rows, w_gate, w_up, (0, half)),
-        hidden_of(place, near_rows, w_gate, w_up, (half, units)),
+        hidden_of(place, near_rows, w_gate, w_up, (0, half)), hidden_of(place, near_rows, w_gate, w_up, (half, units))
     ]
-    pieces = returned(FAR, far_terms)
-    near_terms = reduced(NEAR, near_hidden)
-    pieces.update(returned(NEAR, near_terms))
+    pieces = [[] for _ in range(EXPERTS)]
+    for i, d in enumerate(FAR):
+        start = i * CAP
+        terms, starts = list(far_terms[0]), [start] * len(far_terms[0])
+        for s in range(1, members):
+            (total,) = add_rows(far_terms[s], [[start] * len(far_terms[s])])
+            terms.append(to_member(total, members - s))
+            starts.append(0)
+        (total,) = add_rows(terms, [starts])
+        pieces[d].append(to_expert(total, d))
+    (near_terms,) = reduced(near_hidden, [CAP * len(NEAR) * members])
+    slots = [(s, i) for s in groups for i in range(len(NEAR))]
+    starts = [[(s * len(NEAR) + i) * CAP] * len(near_terms) for s, i in slots]
+    for (s, i), total in zip(slots, add_rows(near_terms, starts)):
+        d = NEAR[i]
+        if s or d:
+            total = send(total, lambda e, m, t, d=d, s=s: (e ^ d, (m + members - s) % members, t))
+        pieces[d].append(total)
     picks, weights = plan(place, routes_t, weight_t)
-    return mix(weights, picks, [pieces[d] for d in range(EXPERTS)])
+    return mix(weights, picks, pieces)
 
 
 def solution(mesh):

time: 84.1 us -> 71.8 us (0.85)
  Pallas kernels: 50.3 us -> 36.1 us
  waiting for transfers between devices: 5.59 us -> 14.8 us
  local copies, waits for them, and re-layouts: 5.26 us -> 0.87 us
  starting transfers between devices: 22.4 us -> 19.5 us
    pallas_call x12 -> x9, Pallas kernels: 29.2 us -> 14 us  [the longest x3 12.4 us: dequant(): pl.pallas_call(functools.partial(dequant_kernel, step, ahead), in_specs=[...]
    ppermute x22 -> x19, waiting for transfers between devices: 5.59 us -> 14.8 us  [send(): return lax.ppermute(x, ('ep', 'tp'), pairs)]
    unnamed x8 -> x20, local copies, waits for them, and re-layouts: 5.26 us -> 0.87 us
    ppermute x22 -> x19, starting transfers between devices: 22.4 us -> 19.5 us  [send(): return lax.ppermute(x, ('ep', 'tp'), pairs)]
  transfers between devices with their start and end apart: 22 -> 19, of which waited for: 3 -> 7; matrix products, arithmetic and copies ran while one was open for 0% -> 0% of each run, Pallas kernels for 56% -> 44%
where the time goes in v1:
time: 71.8 us; the launch traced here: 71.6 us
  Pallas kernels  36.1 us (50%)
  starting transfers between devices  19.5 us (27%)
  waiting for transfers between devices  14.8 us (21%)
  local copies, waits for them, and re-layouts  0.87 us (1%)
    ppermute x19, starting transfers between devices, send(): return lax.ppermute(x, ('ep', 'tp'), pairs)  19.5 us
    ppermute x19, waiting for transfers between devices, send(): return lax.ppermute(x, ('ep', 'tp'), pairs)  14.8 us
    pallas_call x3, Pallas kernels, dequant(): pl.pallas_call(functools.partial(dequant_kernel, step, ahead), in_specs=[...  12.4 us
    pallas_call x3, Pallas kernels, hidden_of(): pl.pallas_call(functools.partial(hidden_kernel, parts, len(xs), span), in...  11 us
    pallas_call x4, Pallas kernels, down(): pl.pallas_call(functools.partial(down_kernel, len(hs), shift, parts), in_...  7.13 us
    pallas_call x1, Pallas kernels, pack(): pl.pallas_call(pack_kernel, grid_spec=pltpu.PrefetchScalarGridSpec(num_sc...  2.92 us
  transfers between devices with their start and end apart: 19, of which 7 were waited for; matrix products, arithmetic and copies ran while one was open for 0% of the time, Pallas kernels for 44%

profile of v1, /device:TPU:0, one launch (start us, length us, event | category | flops | bytes accessed | tf_op | source)
XLA Modules:
  0.0 71.6 jit_solution(9879880484340903123)
XLA Ops:
  0.1 0.8 %copy-done.4 = s32[64,2]{0,1:T(2,128)S(1)} copy-done((s32[64,2]{0,1:T(2,128)S(1)}, s32[64,2]{0,1:T(2,128)}, u32[]{:S(2)}) %copy-start.4) | copy-done | bytes 536
  0.9 2.9 %pack.1 = (bf16[40,1536]{1,0:T(8,128)(2,1)S(1)}, bf16[40,1536]{1,0:T(8,128)(2,1)S(1)}, bf16[40,1536]{1,0:T(8,128)(2,1)S(1)}, bf16[40,1536]{1,0:T(8,128)(2,1)S(1)}) custom-call(s32[2]{0:T(128)S(1)} %pad_add_fusion.place, s32[2,64]{1,0:T(2,128)S(1)} %bitcast.12, bf16[64,3072]{1,0:T(8,128)(2,1)} %tokens_ref.1), custom_call_target="tpu_custom_call" | custom-call | flops 6000000000 | tf_op jit(solution)/shard_map/pack/pallas_call | solution.py:57
  3.8 5.1 %collective-permute-start.8 = (bf16[40,1536]{1,0:T(8,128)(2,1)S(1)}, bf16[40,1536]{1,0:T(8,128)(2,1)S(1)}, u32[]{:S(2)}, u32[]{:S(2)}) collective-permute-start(bf16[40,1536]{1,0:T(8,128)(2,1)S(1)} %get-tuple-element.33), channel_id=1, source_target_pairs={{0,12},{1,13},{2,14},{3,15},{4,8},{5,9},{6,10},{7,11},{8,4},{9,5},... | collective-permute-start | bytes 368648 | tf_op jit(solution)/shard_map/ppermute | solution.py:319
  9.0 0.6 collective-permute-start
  9.6 3.3 %shard_map.92.refs_4_ = bf16[3072,2048]{1,0:T(8,128)(2,1)S(1)} custom-call(bf16[3072,2048]{1,0:T(8,128)(2,1)S(1)} %copy-done, f32[16,3072]{1,0:T(8,128)S(1)} %bitcast.9), custom_call_target="tpu_custom_call" | custom-call | flops 5000000000 | bytes 12582912 | tf_op jit(solution)/shard_map/pallas_call | solution.py:118
  12.9 3.9 %collective-permute-done.refs_0_ = bf16[40,1536]{1,0:T(8,128)(2,1)S(1)} collective-permute-done((bf16[40,1536]{1,0:T(8,128)(2,1)S(1)}, bf16[40,1536]{1,0:T(8,128)(2,1)S(1)}, u32[]{:S(2)}, u32[]{:S(2)}) %collective-permute-start) | collective-permute-done | bytes 122912 | tf_op jit(solution)/shard_map/ppermute | solution.py:319
  16.9 1.6 %collective-permute-start.2 = (bf16[80,1536]{1,0:T(8,128)(2,1)S(1)}, bf16[80,1536]{1,0:T(8,128)(2,1)S(1)}, u32[]{:S(2)}, u32[]{:S(2)}) collective-permute-start(bf16[80,1536]{1,0:T(8,128)(2,1)S(1)} %shard_map.91.refs_0_), channel_id=1, source_target_pairs={{0,2},{1,3},{2,0},{3,1},{4,6},{5,7},{6,4},{7,5},{8,10},{9,11},{10,... | collective-permute-start | bytes 737288 | tf_op jit(solution)/shard_map/ppermute | solution.py:319
  18.5 3.3 %shard_map.93.refs_5_ = bf16[3072,2048]{1,0:T(8,128)(2,1)S(1)} custom-call(bf16[3072,2048]{1,0:T(8,128)(2,1)S(1)} %bitcast.8, f32[16,3072]{1,0:T(8,128)S(1)} %bitcast.10), custom_call_target="tpu_custom_call" | custom-call | flops 5000000000 | bytes 12582912 | tf_op jit(solution)/shard_map/pallas_call | solution.py:118
  22.0 0.6 collective-permute-start.11
  22.5 1.3 %collective-permute-done.2.refs_2_ = bf16[80,1536]{1,0:T(8,128)(2,1)S(1)} collective-permute-done((bf16[80,1536]{1,0:T(8,128)(2,1)S(1)}, bf16[80,1536]{1,0:T(8,128)(2,1)S(1)}, u32[]{:S(2)}, u32[]{:S(2)}) %collective-permute-start.2) | collective-permute-done | bytes 245792 | tf_op jit(solution)/shard_map/ppermute | solution.py:319
  23.8 5.8 %shard_map.96.refs_2_.refs_1_ = bf16[2048,3072]{1,0:T(8,128)(2,1)S(1)} custom-call(bf16[2048,3072]{1,0:T(8,128)(2,1)} %code.5, f32[24,2048]{1,0:T(8,128)S(1)} %bitcast.11), custom_call_target="tpu_custom_call" | custom-call | flops 5000000000 | bytes 12582912 | tf_op jit(solution)/shard_map/pallas_call | solution.py:118
  29.6 0.6 collective-permute-start.10
  30.4 3.1 %shard_map.95.refs_1_ = bf16[160,1024]{1,0:T(8,128)(2,1)S(1)} custom-call(s32[2]{0:T(128)S(1)} %pad_add_fusion.place, bf16[80,1536]{1,0:T(8,128)(2,1)S(1)} %shard_map.91.refs_0_, bf16[80,1536]{1,0:T(8,128)(2,1)S(1)} %collective-permute-done.1.refs_1_, bf16[80,1536]{1,0:T(8,128)(2,1)S(1)} %collective-permute-done.2.refs_2_, ...), custom_call_target="tpu_custom_call" | custom-call | flops 2013265920 | tf_op jit(solution)/shard_map/pallas_call | solution.py:163
  33.5 2.9 %shard_map.94.refs_0_ = bf16[160,1024]{1,0:T(8,128)(2,1)S(1)} custom-call(s32[2]{0:T(128)S(1)} %pad_add_fusion.place, bf16[80,1536]{1,0:T(8,128)(2,1)S(1)} %shard_map.91.refs_0_, bf16[80,1536]{1,0:T(8,128)(2,1)S(1)} %collective-permute-done.1.refs_1_, bf16[80,1536]{1,0:T(8,128)(2,1)S(1)} %collective-permute-done.2.refs_2_, ...), custom_call_target="tpu_custom_call" | custom-call | flops 2013265920 | tf_op jit(solution)/shard_map/pallas_call | solution.py:163
  36.4 1.8 %shard_map.97 = bf16[160,1536]{1,0:T(8,128)(2,1)S(1)} custom-call(s32[2]{0:T(128)S(1)} %pad_add_fusion.place, bf16[160,1024]{1,0:T(8,128)(2,1)S(1)} %shard_map.94.refs_0_, bf16[160,1024]{1,0:T(8,128)(2,1)S(1)} %shard_map.95.refs_1_, bf16[2048,3072]{1,0:T(8,128)(2,1)S(1)} %shard_map.96.refs_2_.refs_1_), custom_call_target="tpu_custom_call" | custom-call | flops 1006632960 | tf_op jit(solution)/shard_map/pallas_call | solution.py:198
  38.2 0.6 collective-permute-start.4
  38.7 5.1 %shard_map.101.refs_0_ = bf16[160,2048]{1,0:T(8,128)(2,1)S(1)} custom-call(s32[2]{0:T(128)S(1)} %pad_add_fusion.place, bf16[80,1536]{1,0:T(8,128)(2,1)S(1)} %shard_map.100.refs_0_, bf16[80,1536]{1,0:T(8,128)(2,1)S(1)} %collective-permute-done.10.refs_1_, bf16[80,1536]{1,0:T(8,128)(2,1)S(1)} %collective-permute-done.11.refs_2_, ...), custom_call_target="tpu_custom_call" | custom-call | flops 4026531840 | tf_op jit(solution)/shard_map/pallas_call | solution.py:163
  43.8 1.8 %shard_map.102 = (bf16[80,1536]{1,0:T(8,128)(2,1)S(1)}, bf16[80,1536]{1,0:T(8,128)(2,1)S(1)}) custom-call(s32[2]{0:T(128)S(1)} %pad_add_fusion.place, bf16[160,2048]{1,0:T(8,128)(2,1)S(1)} %shard_map.101.refs_0_, bf16[2048,3072]{1,0:T(8,128)(2,1)S(1)} %shard_map.96.refs_2_.refs_1_), custom_call_target="tpu_custom_call" | custom-call | flops 1006632960 | tf_op jit(solution)/shard_map/pallas_call | solution.py:198
  45.7 0.5 collective-permute-start.13
  46.2 1.8 %shard_map.103 = (f32[80,1536]{1,0:T(8,128)S(1)}, f32[80,1536]{1,0:T(8,128)S(1)}) custom-call(s32[2]{0:T(128)S(1)} %pad_add_fusion.place, bf16[160,2048]{1,0:T(8,128)(2,1)S(1)} %shard_map.101.refs_0_, bf16[2048,3072]{1,0:T(8,128)(2,1)S(1)} %shard_map.96.refs_2_.refs_1_), custom_call_target="tpu_custom_call" | custom-call | flops 1006632960 | tf_op jit(solution)/shard_map/pallas_call | solution.py:198
  48.0 1.4 %collective-permute-start.17 = (bf16[40,1536]{1,0:T(8,128)(2,1)S(1)}, bf16[40,1536]{1,0:T(8,128)(2,1)S(1)}, u32[]{:S(2)}, u32[]{:S(2)}) collective-permute-start(bf16[40,1536]{1,0:T(8,128)(2,1)S(1)} %shard_map.106), channel_id=1, source_target_pairs={{0,2},{1,3},{2,0},{3,1},{4,6},{5,7},{6,4},{7,5},{8,10},{9,11},{10,... | collective-permute-start | bytes 368648 | tf_op jit(solution)/shard_map/ppermute | solution.py:319
  49.4 0.8 %collective-permute-start.15 = (bf16[40,1536]{1,0:T(8,128)(2,1)S(1)}, bf16[40,1536]{1,0:T(8,128)(2,1)S(1)}, u32[]{:S(2)}, u32[]{:S(2)}) collective-permute-start(bf16[40,1536]{1,0:T(8,128)(2,1)S(1)} %shard_map.104), channel_id=1, source_target_pairs={{0,2},{1,3},{2,0},{3,1},{4,6},{5,7},{6,4},{7,5},{8,10},{9,11},{10,... | collective-permute-start | bytes 368648 | tf_op jit(solution)/shard_map/ppermute | solution.py:319
  50.2 1.8 %shard_map.98.refs_1_ = f32[160,1536]{1,0:T(8,128)S(1)} custom-call(s32[2]{0:T(128)S(1)} %pad_add_fusion.place, bf16[160,1024]{1,0:T(8,128)(2,1)S(1)} %shard_map.94.refs_0_, bf16[160,1024]{1,0:T(8,128)(2,1)S(1)} %shard_map.95.refs_1_, bf16[2048,3072]{1,0:T(8,128)(2,1)S(1)} %shard_map.96.refs_2_.refs_1_), custom_call_target="tpu_custom_call" | custom-call | flops 1006632960 | tf_op jit(solution)/shard_map/pallas_call | solution.py:198
  52.0 2.3 %collective-permute-done.17.refs_2_ = bf16[40,1536]{1,0:T(8,128)(2,1)S(1)} collective-permute-done((bf16[40,1536]{1,0:T(8,128)(2,1)S(1)}, bf16[40,1536]{1,0:T(8,128)(2,1)S(1)}, u32[]{:S(2)}, u32[]{:S(2)}) %collective-permute-start.17) | collective-permute-done | bytes 122912 | tf_op jit(solution)/shard_map/ppermute | solution.py:319
  54.3 3.1 %collective-permute-start.18 = (bf16[40,1536]{1,0:T(8,128)(2,1)S(1)}, bf16[40,1536]{1,0:T(8,128)(2,1)S(1)}, u32[]{:S(2)}, u32[]{:S(2)}) collective-permute-start(bf16[40,1536]{1,0:T(8,128)(2,1)S(1)} %shard_map.107), channel_id=1, source_target_pairs={{0,12},{1,13},{2,14},{3,15},{4,8},{5,9},{6,10},{7,11},{8,4},{9,5},... | collective-permute-start | bytes 368648 | tf_op jit(solution)/shard_map/ppermute | solution.py:319
  57.5 1.0 %collective-permute-start.16 = (bf16[40,1536]{1,0:T(8,128)(2,1)S(1)}, bf16[40,1536]{1,0:T(8,128)(2,1)S(1)}, u32[]{:S(2)}, u32[]{:S(2)}) collective-permute-start(bf16[40,1536]{1,0:T(8,128)(2,1)S(1)} %shard_map.105), channel_id=1, source_target_pairs={{0,8},{1,9},{2,10},{3,11},{4,12},{5,13},{6,14},{7,15},{8,0},{9,1},... | collective-permute-start | bytes 368648 | tf_op jit(solution)/shard_map/ppermute | solution.py:319
  58.5 1.4 %collective-permute-start.5 = (bf16[40,1536]{1,0:T(8,128)(2,1)S(1)}, bf16[40,1536]{1,0:T(8,128)(2,1)S(1)}, u32[]{:S(2)}, u32[]{:S(2)}) collective-permute-start(bf16[40,1536]{1,0:T(8,128)(2,1)S(1)} %get-tuple-element.30), channel_id=1, source_target_pairs={{0,2},{1,3},{2,0},{3,1},{4,6},{5,7},{6,4},{7,5},{8,10},{9,11},{10,... | collective-permute-start | bytes 368648 | tf_op jit(solution)/shard_map/ppermute | solution.py:319
  60.0 2.0 %collective-permute-start.6 = (bf16[40,1536]{1,0:T(8,128)(2,1)S(1)}, bf16[40,1536]{1,0:T(8,128)(2,1)S(1)}, u32[]{:S(2)}, u32[]{:S(2)}) collective-permute-start(bf16[40,1536]{1,0:T(8,128)(2,1)S(1)} %get-tuple-element.31), channel_id=1, source_target_pairs={{0,4},{1,5},{2,6},{3,7},{4,0},{5,1},{6,2},{7,3},{8,12},{9,13},{10,... | collective-permute-start | bytes 368648 | tf_op jit(solution)/shard_map/ppermute | solution.py:319
  62.1 1.0 %plan.1 = (bf16[128,40]{1,0:T(8,128)(2,1)S(1)}, bf16[128,40]{1,0:T(8,128)(2,1)S(1)}, bf16[128,40]{1,0:T(8,128)(2,1)S(1)}, bf16[128,40]{1,0:T(8,128)(2,1)S(1)}, f32[64,2]{1,0:T(8,128)S(1)}) custom-call(s32[2]{0:T(128)S(1)} %pad_add_fusion.place, s32[2,64]{1,0:T(2,128)S(1)} %bitcast.13, f32[2,64]{1,0:T(2,128)S(1)} %bitcast.14), custom_call_target="tpu_custom_call" | custom-call | tf_op jit(solution)/shard_map/plan/pallas_call | solution.py:265
  63.1 4.8 %collective-permute-done.16.refs_9_ = bf16[40,1536]{1,0:T(8,128)(2,1)S(1)} collective-permute-done((bf16[40,1536]{1,0:T(8,128)(2,1)S(1)}, bf16[40,1536]{1,0:T(8,128)(2,1)S(1)}, u32[]{:S(2)}, u32[]{:S(2)}) %collective-permute-start.16) | collective-permute-done | bytes 122912 | tf_op jit(solution)/shard_map/ppermute | solution.py:319
  68.0 2.1 %collective-permute-done.7.refs_8_ = bf16[40,1536]{1,0:T(8,128)(2,1)S(1)} collective-permute-done((bf16[40,1536]{1,0:T(8,128)(2,1)S(1)}, bf16[40,1536]{1,0:T(8,128)(2,1)S(1)}, u32[]{:S(2)}, u32[]{:S(2)}) %collective-permute-start.7) | collective-permute-done | bytes 122912 | tf_op jit(solution)/shard_map/ppermute | solution.py:319
  70.2 1.4 %mix.1 = bf16[64,1536]{1,0:T(8,128)(2,1)} custom-call(f32[64,2]{1,0:T(8,128)S(1)} %get-tuple-element.22.refs_0_, bf16[128,40]{1,0:T(8,128)(2,1)S(1)} %get-tuple-element.23.refs_1_, bf16[128,40]{1,0:T(8,128)(2,1)S(1)} %get-tuple-element.24.refs_2_, bf16[128,40]{1,0:T(8,128)(2,1)S(1)} %get-tuple-element.25.refs_3_, ...), custom_call_target="tpu_custom_call" | custom-call | tf_op jit(solution)/shard_map/mix/pallas_call | solution.py:295
  (48 shorter events, 1.1 us)
Async XLA Ops:
  0.0 9.6 %copy-start.1 = (f32[3072,16]{0,1:T(8,128)S(1)}, f32[3072,16]{0,1:T(8,128)}, u32[]{:S(2)}) copy-start(f32[3072,16]{0,1:T(8,128)} %param.13) | copy-start | bytes 589828
  0.0 9.6 %copy-start = (bf16[3072,2048]{1,0:T(8,128)(2,1)S(1)}, bf16[3072,2048]{1,0:T(8,128)(2,1)}, u32[]{:S(2)}) copy-start(bf16[3072,2048]{1,0:T(8,128)(2,1)} %code.3) | copy-start | bytes 37748740
  0.1 0.8 %copy-start.4 = (s32[64,2]{0,1:T(2,128)S(1)}, s32[64,2]{0,1:T(2,128)}, u32[]{:S(2)}) copy-start(s32[64,2]{0,1:T(2,128)} %param.10) | copy-start | bytes 1540
  0.9 17.6 %slice-start = ((s8[12582912]{0:T(1024)(128)(4,1)}), s8[4194304]{0:T(1024)(128)(4,1)S(1)}, s32[]{:S(2)}) async-start(s8[12582912]{0:T(1024)(128)(4,1)} %bitcast.7), calls=%async_computation | async-start | bytes 8388608
  0.9 17.6 %slice-start.1 = ((s8[12582912]{0:T(1024)(128)(4,1)}), s8[4194304]{0:T(1024)(128)(4,1)S(1)}, s32[]{:S(2)}) async-start(s8[12582912]{0:T(1024)(128)(4,1)} %bitcast.7), calls=%async_computation.1 | async-start | bytes 8388608
  3.8 18.1 %collective-permute-start.8 = (bf16[40,1536]{1,0:T(8,128)(2,1)S(1)}, bf16[40,1536]{1,0:T(8,128)(2,1)S(1)}, u32[]{:S(2)}, u32[]{:S(2)}) collective-permute-start(bf16[40,1536]{1,0:T(8,128)(2,1)S(1)} %get-tuple-element.33), channel_id=1, source_target_pairs={{0,12},{1,13},{2,14},{3,15},{4,8},{5,9},{6,10},{7,11},{8,4},{9,5},... | collective-permute-start | bytes 368648 | tf_op jit(solution)/shard_map/ppermute | solution.py:319
  9.0 13.0 %collective-permute-start.9 = (bf16[40,1536]{1,0:T(8,128)(2,1)S(1)}, bf16[40,1536]{1,0:T(8,128)(2,1)S(1)}, u32[]{:S(2)}, u32[]{:S(2)}) collective-permute-start(bf16[40,1536]{1,0:T(8,128)(2,1)S(1)} %get-tuple-element.34), channel_id=1, source_target_pairs={{0,8},{1,9},{2,10},{3,11},{4,12},{5,13},{6,14},{7,15},{8,0},{9,1},... | collective-permute-start | bytes 368648 | tf_op jit(solution)/shard_map/ppermute | solution.py:319
  9.0 7.9 %collective-permute-start = (bf16[40,1536]{1,0:T(8,128)(2,1)S(1)}, bf16[40,1536]{1,0:T(8,128)(2,1)S(1)}, u32[]{:S(2)}, u32[]{:S(2)}) collective-permute-start(bf16[40,1536]{1,0:T(8,128)(2,1)S(1)} %get-tuple-element.27), channel_id=1, source_target_pairs={{0,4},{1,5},{2,6},{3,7},{4,0},{5,1},{6,2},{7,3},{8,12},{9,13},{10,... | collective-permute-start | bytes 368648 | tf_op jit(solution)/shard_map/ppermute | solution.py:319
  9.6 8.9 %slice-start.2 = ((s8[12582912]{0:T(1024)(128)(4,1)}), s8[4194304]{0:T(1024)(128)(4,1)S(1)}, s32[]{:S(2)}) async-start(s8[12582912]{0:T(1024)(128)(4,1)} %bitcast.7), calls=%async_computation.2 | async-start | bytes 8388608
  9.6 8.9 %copy-start.2 = (f32[3072,16]{0,1:T(8,128)S(1)}, f32[3072,16]{0,1:T(8,128)}, u32[]{:S(2)}) copy-start(f32[3072,16]{0,1:T(8,128)} %param.15) | copy-start | bytes 589828
  16.9 6.9 %collective-permute-start.2 = (bf16[80,1536]{1,0:T(8,128)(2,1)S(1)}, bf16[80,1536]{1,0:T(8,128)(2,1)S(1)}, u32[]{:S(2)}, u32[]{:S(2)}) collective-permute-start(bf16[80,1536]{1,0:T(8,128)(2,1)S(1)} %shard_map.91.refs_0_), channel_id=1, source_target_pairs={{0,2},{1,3},{2,0},{3,1},{4,6},{5,7},{6,4},{7,5},{8,10},{9,11},{10,... | collective-permute-start | bytes 737288 | tf_op jit(solution)/shard_map/ppermute | solution.py:319
  18.5 5.3 %copy-start.3 = (f32[2048,24]{0,1:T(8,128)S(1)}, f32[2048,24]{0,1:T(8,128)}, u32[]{:S(2)}) copy-start(f32[2048,24]{0,1:T(8,128)} %param.17) | copy-start | bytes 589828
  21.8 8.5 %collective-permute-start.1 = (bf16[80,1536]{1,0:T(8,128)(2,1)S(1)}, bf16[80,1536]{1,0:T(8,128)(2,1)S(1)}, u32[]{:S(2)}, u32[]{:S(2)}) collective-permute-start(bf16[80,1536]{1,0:T(8,128)(2,1)S(1)} %shard_map.91.refs_0_), channel_id=1, source_target_pairs={{0,1},{1,0},{2,3},{3,2},{4,5},{5,4},{6,7},{7,6},{8,9},{9,8},{10,11... | collective-permute-start | bytes 737288 | tf_op jit(solution)/shard_map/ppermute | solution.py:319
  22.0 8.4 %collective-permute-start.11 = (bf16[80,1536]{1,0:T(8,128)(2,1)S(1)}, bf16[80,1536]{1,0:T(8,128)(2,1)S(1)}, u32[]{:S(2)}, u32[]{:S(2)}) collective-permute-start(bf16[80,1536]{1,0:T(8,128)(2,1)S(1)} %shard_map.100.refs_0_), channel_id=1, source_target_pairs={{0,2},{1,3},{2,0},{3,1},{4,6},{5,7},{6,4},{7,5},{8,10},{9,11},{10,... | collective-permute-start | bytes 737288 | tf_op jit(solution)/shard_map/ppermute | solution.py:319
  23.8 6.5 %collective-permute-start.3 = (bf16[80,1536]{1,0:T(8,128)(2,1)S(1)}, bf16[80,1536]{1,0:T(8,128)(2,1)S(1)}, u32[]{:S(2)}, u32[]{:S(2)}) collective-permute-start(bf16[80,1536]{1,0:T(8,128)(2,1)S(1)} %collective-permute-done.2.refs_2_), channel_id=1, source_target_pairs={{0,1},{1,0},{2,3},{3,2},{4,5},{5,4},{6,7},{7,6},{8,9},{9,8},{10,11... | collective-permute-start | bytes 737288 | tf_op jit(solution)/shard_map/ppermute | solution.py:319
  29.6 9.1 %collective-permute-start.10 = (bf16[80,1536]{1,0:T(8,128)(2,1)S(1)}, bf16[80,1536]{1,0:T(8,128)(2,1)S(1)}, u32[]{:S(2)}, u32[]{:S(2)}) collective-permute-start(bf16[80,1536]{1,0:T(8,128)(2,1)S(1)} %shard_map.100.refs_0_), channel_id=1, source_target_pairs={{0,1},{1,0},{2,3},{3,2},{4,5},{5,4},{6,7},{7,6},{8,9},{9,8},{10,11... | collective-permute-start | bytes 737288 | tf_op jit(solution)/shard_map/ppermute | solution.py:319
  30.4 8.4 %collective-permute-start.12 = (bf16[80,1536]{1,0:T(8,128)(2,1)S(1)}, bf16[80,1536]{1,0:T(8,128)(2,1)S(1)}, u32[]{:S(2)}, u32[]{:S(2)}) collective-permute-start(bf16[80,1536]{1,0:T(8,128)(2,1)S(1)} %collective-permute-done.11.refs_2_), channel_id=1, source_target_pairs={{0,1},{1,0},{2,3},{3,2},{4,5},{5,4},{6,7},{7,6},{8,9},{9,8},{10,11... | collective-permute-start | bytes 737288 | tf_op jit(solution)/shard_map/ppermute | solution.py:319
  38.2 20.3 %collective-permute-start.4 = (bf16[160,1536]{1,0:T(8,128)(2,1)S(1)}, bf16[160,1536]{1,0:T(8,128)(2,1)S(1)}, u32[]{:S(2)}, u32[]{:S(2)}) collective-permute-start(bf16[160,1536]{1,0:T(8,128)(2,1)S(1)} %shard_map.97), channel_id=1, source_target_pairs={{0,1},{1,0},{2,3},{3,2},{4,5},{5,4},{6,7},{7,6},{8,9},{9,8},{10,11... | collective-permute-start | bytes 1474568 | tf_op jit(solution)/shard_map/ppermute | solution.py:319
  45.6 2.4 %collective-permute-start.14 = (bf16[80,1536]{1,0:T(8,128)(2,1)S(1)}, bf16[80,1536]{1,0:T(8,128)(2,1)S(1)}, u32[]{:S(2)}, u32[]{:S(2)}) collective-permute-start(bf16[80,1536]{1,0:T(8,128)(2,1)S(1)} %get-tuple-element.37), channel_id=1, source_target_pairs={{0,1},{1,0},{2,3},{3,2},{4,5},{5,4},{6,7},{7,6},{8,9},{9,8},{10,11... | collective-permute-start | bytes 737288 | tf_op jit(solution)/shard_map/ppermute | solution.py:319
  45.7 6.3 %collective-permute-start.13 = (bf16[80,1536]{1,0:T(8,128)(2,1)S(1)}, bf16[80,1536]{1,0:T(8,128)(2,1)S(1)}, u32[]{:S(2)}, u32[]{:S(2)}) collective-permute-start(bf16[80,1536]{1,0:T(8,128)(2,1)S(1)} %get-tuple-element.35), channel_id=1, source_target_pairs={{0,1},{1,0},{2,3},{3,2},{4,5},{5,4},{6,7},{7,6},{8,9},{9,8},{10,11... | collective-permute-start | bytes 737288 | tf_op jit(solution)/shard_map/ppermute | solution.py:319
  48.0 14.1 %copy-start.5 = (s32[64,2]{0,1:T(2,128)S(1)}, s32[64,2]{0,1:T(2,128)}, u32[]{:S(2)}) copy-start(s32[64,2]{0,1:T(2,128)} %param.10) | copy-start | bytes 1540
  48.0 14.1 %copy-start.6 = (f32[64,2]{0,1:T(2,128)S(1)}, f32[64,2]{0,1:T(2,128)}, u32[]{:S(2)}) copy-start(f32[64,2]{0,1:T(2,128)} %param.11) | copy-start | bytes 1540
  48.0 6.3 %collective-permute-start.17 = (bf16[40,1536]{1,0:T(8,128)(2,1)S(1)}, bf16[40,1536]{1,0:T(8,128)(2,1)S(1)}, u32[]{:S(2)}, u32[]{:S(2)}) collective-permute-start(bf16[40,1536]{1,0:T(8,128)(2,1)S(1)} %shard_map.106), channel_id=1, source_target_pairs={{0,2},{1,3},{2,0},{3,1},{4,6},{5,7},{6,4},{7,5},{8,10},{9,11},{10,... | collective-permute-start | bytes 368648 | tf_op jit(solution)/shard_map/ppermute | solution.py:319
  49.4 8.0 %collective-permute-start.15 = (bf16[40,1536]{1,0:T(8,128)(2,1)S(1)}, bf16[40,1536]{1,0:T(8,128)(2,1)S(1)}, u32[]{:S(2)}, u32[]{:S(2)}) collective-permute-start(bf16[40,1536]{1,0:T(8,128)(2,1)S(1)} %shard_map.104), channel_id=1, source_target_pairs={{0,2},{1,3},{2,0},{3,1},{4,6},{5,7},{6,4},{7,5},{8,10},{9,11},{10,... | collective-permute-start | bytes 368648 | tf_op jit(solution)/shard_map/ppermute | solution.py:319
  54.3 8.7 %collective-permute-start.18 = (bf16[40,1536]{1,0:T(8,128)(2,1)S(1)}, bf16[40,1536]{1,0:T(8,128)(2,1)S(1)}, u32[]{:S(2)}, u32[]{:S(2)}) collective-permute-start(bf16[40,1536]{1,0:T(8,128)(2,1)S(1)} %shard_map.107), channel_id=1, source_target_pairs={{0,12},{1,13},{2,14},{3,15},{4,8},{5,9},{6,10},{7,11},{8,4},{9,5},... | collective-permute-start | bytes 368648 | tf_op jit(solution)/shard_map/ppermute | solution.py:319
  57.5 10.4 %collective-permute-start.16 = (bf16[40,1536]{1,0:T(8,128)(2,1)S(1)}, bf16[40,1536]{1,0:T(8,128)(2,1)S(1)}, u32[]{:S(2)}, u32[]{:S(2)}) collective-permute-start(bf16[40,1536]{1,0:T(8,128)(2,1)S(1)} %shard_map.105), channel_id=1, source_target_pairs={{0,8},{1,9},{2,10},{3,11},{4,12},{5,13},{6,14},{7,15},{8,0},{9,1},... | collective-permute-start | bytes 368648 | tf_op jit(solution)/shard_map/ppermute | solution.py:319
  58.5 9.3 %collective-permute-start.5 = (bf16[40,1536]{1,0:T(8,128)(2,1)S(1)}, bf16[40,1536]{1,0:T(8,128)(2,1)S(1)}, u32[]{:S(2)}, u32[]{:S(2)}) collective-permute-start(bf16[40,1536]{1,0:T(8,128)(2,1)S(1)} %get-tuple-element.30), channel_id=1, source_target_pairs={{0,2},{1,3},{2,0},{3,1},{4,6},{5,7},{6,4},{7,5},{8,10},{9,11},{10,... | collective-permute-start | bytes 368648 | tf_op jit(solution)/shard_map/ppermute | solution.py:319
  60.0 8.1 %collective-permute-start.6 = (bf16[40,1536]{1,0:T(8,128)(2,1)S(1)}, bf16[40,1536]{1,0:T(8,128)(2,1)S(1)}, u32[]{:S(2)}, u32[]{:S(2)}) collective-permute-start(bf16[40,1536]{1,0:T(8,128)(2,1)S(1)} %get-tuple-element.31), channel_id=1, source_target_pairs={{0,4},{1,5},{2,6},{3,7},{4,0},{5,1},{6,2},{7,3},{8,12},{9,13},{10,... | collective-permute-start | bytes 368648 | tf_op jit(solution)/shard_map/ppermute | solution.py:319
  61.9 8.2 %collective-permute-start.7 = (bf16[40,1536]{1,0:T(8,128)(2,1)S(1)}, bf16[40,1536]{1,0:T(8,128)(2,1)S(1)}, u32[]{:S(2)}, u32[]{:S(2)}) collective-permute-start(bf16[40,1536]{1,0:T(8,128)(2,1)S(1)} %get-tuple-element.32), channel_id=1, source_target_pairs={{0,6},{1,7},{2,4},{3,5},{4,2},{5,3},{6,0},{7,1},{8,14},{9,15},{10,... | collective-permute-start | bytes 368648 | tf_op jit(solution)/shard_map/ppermute | solution.py:319

commit v2 on v1

--- a/solution.py
+++ b/solution.py
@@ -1,4 +1,5 @@
 import functools
+import math
 
 import jax
 import jax.numpy as jnp
@@ -38,15 +39,25 @@
     return named, jnp.dot(wide, earlier, preferred_element_type=F32)[0:1, :]
 
 
-def pack_kernel(place, routes_ref, tokens_ref, *outs):
+def pack_kernel(place, routes_hbm, tokens_hbm, *refs):
+    *outs, routes_ref, tokens_ref, sems = refs
     own = place[0]
+    count, part = tokens_ref.shape
+    cols = pl.ds(pl.multiple_of(place[1] * part, part), part)
+    routes_copy = pltpu.make_async_copy(routes_hbm, routes_ref, sems.at[0])
+    tokens_copy = pltpu.make_async_copy(tokens_hbm.at[:, cols], tokens_ref, sems.at[1])
+    routes_copy.start()
+    tokens_copy.start()
+    routes_copy.wait()
     routes_t = routes_ref[...]
-    count = routes_t.shape[1]
     slots = lax.broadcasted_iota(jnp.int32, (CAP, count), 0)
-    for d, out in enumerate(outs):
+    picks = []
+    for d in range(len(outs)):
         named, rank = ranks(routes_t, own ^ d)
         hit = (slots == rank.astype(jnp.int32)) & (jnp.broadcast_to(named, (CAP, count)) > 0.5)
-        picked = jnp.where(hit, 1.0, 0.0).astype(BF16)
+        picks.append(jnp.where(hit, 1.0, 0.0).astype(BF16))
+    tokens_copy.wait()
+    for picked, out in zip(picks, outs):
         out[...] = jnp.dot(picked, tokens_ref[...], preferred_element_type=F32).astype(BF16)
 
 
@@ -54,33 +65,38 @@
     count, width = tokens.shape
     part = width // parts
     tokens = pltpu.with_memory_space_constraint(tokens, pltpu.HBM)
+    routes_t = pltpu.with_memory_space_constraint(routes_t, pltpu.HBM)
+    in_hbm = pl.BlockSpec(memory_space=pltpu.HBM)
     return pl.pallas_call(
         pack_kernel,
-        grid_spec=pltpu.PrefetchScalarGridSpec(
-            num_scalar_prefetch=1,
-            grid=(1,),
-            in_specs=[
-                pl.BlockSpec(routes_t.shape, lambda i, place: (0, 0)),
-                pl.BlockSpec((count, part), lambda i, place: (0, place[1])),
-            ],
-            out_specs=[pl.BlockSpec((CAP, part), lambda i, place: (0, 0))] * EXPERTS,
-        ),
+        in_specs=[scalar(), in_hbm, in_hbm],
+        out_specs=[whole()] * EXPERTS,
         out_shape=[jax.ShapeDtypeStruct((CAP, part), BF16)] * EXPERTS,
+        scratch_shapes=[VMEM(routes_t.shape, jnp.int32), VMEM((count, part), BF16), pltpu.SemaphoreType.DMA((2,))],
         compiler_params=pltpu.CompilerParams(vmem_limit_bytes=1 * MIB),
         cost_estimate=pl.CostEstimate(flops=6 * 10**9, bytes_accessed=0, transcendentals=0),
         name="pack",
     )(place, routes_t, tokens)
 
 
-def dequant_kernel(step, ahead, code, scale_ref, out, spread, split, column, sems=None):
+def dequant_kernel(step, early, ahead, code, scale_ref, *refs):
+    refs = list(refs)
+    other = refs.pop(0) if early or ahead is not None else None
+    out = refs.pop(0)
+    later = refs.pop(0) if early else None
+    spread, split, column, sems = refs
     rows, _ = out.shape
     blocks = scale_ref.shape[0]
-    pieces = [pl.ds(i * step, step) for i in range(rows // step)]
-    copies = []
-    if ahead:
-        copies = [pltpu.make_async_copy(code.at[at], out.at[at], sems.at[i]) for i, at in enumerate(pieces)]
+
+    def copy_of(piece, source, to):
+        at = pl.ds(piece * step, step)
+        return pltpu.make_async_copy(source.at[at], to.at[at], sems.at[piece])
+
+    copies = [copy_of(i, other, later) for i in range(early)]
+    if ahead is not None:
+        copies = [copy_of(i, code, out) for i in range(ahead, rows // step)]
         code = out
-    for copy in copies[:ahead]:
+    for copy in copies:
         copy.start()
     row = lax.broadcasted_iota(jnp.int32, spread.shape, 0)
     col = lax.broadcasted_iota(jnp.int32, spread.shape, 1)
@@ -90,10 +106,8 @@
     column[...] = scale.T
     split[...] = jnp.concatenate([high, scale - high], axis=0).T.astype(BF16)
     for i in range(rows // step):
-        if ahead:
-            copies[i].wait()
-            if i + ahead < len(copies):
-                copies[i + ahead].start()
+        if ahead is not None and i >= ahead:
+            copies[i - ahead].wait()
         at = slice(i * step, (i + 1) * step)
         for n in range(blocks // 2):
             if n % 4 == 0:
@@ -104,31 +118,45 @@
                 cols = slice(2 * n * QB, 2 * (n + 1) * QB)
                 wide = jnp.dot(split[at, :], spread[:, cols], preferred_element_type=F32)
                 out[at, cols] = (code[at, cols].astype(F32) * wide).astype(BF16)
-
-
-def dequant(code, scale_t, ahead):
+    if ahead is None:
+        for copy in copies:
+            copy.wait()
+
+
+def dequant(code, scale_t, step, following=None, early=0, begun=None):
     rows, width = code.shape
     blocks = scale_t.shape[0]
-    step = min(512, rows)
-    first, sems = whole(), []
-    if ahead:
-        code = pltpu.with_memory_space_constraint(code, pltpu.HBM)
-        first = pl.BlockSpec(memory_space=pltpu.HBM)
-        sems = [pltpu.SemaphoreType.DMA((rows // step,))]
-    return pl.pallas_call(
-        functools.partial(dequant_kernel, step, ahead),
-        in_specs=[first, whole()],
-        out_specs=whole(),
-        out_shape=VMEM((rows, width), BF16),
+    in_hbm = pl.BlockSpec(memory_space=pltpu.HBM)
+    operands, specs = [code, scale_t], [whole(), whole()]
+    outs, aliases = [VMEM((rows, width), BF16)], {}
+    if early and following is not None:
+        operands.append(pltpu.with_memory_space_constraint(following, pltpu.HBM))
+        specs.append(in_hbm)
+        outs.append(VMEM(following.shape, BF16))
+        kernel = functools.partial(dequant_kernel, step, early, None)
+    elif begun is not None:
+        operands[0], specs[0] = pltpu.with_memory_space_constraint(code, pltpu.HBM), in_hbm
+        operands.append(begun)
+        specs.append(whole())
+        aliases = {2: 0}
+        kernel = functools.partial(dequant_kernel, step, 0, early)
+    else:
+        kernel = functools.partial(dequant_kernel, step, 0, None)
+    return pl.pallas_call(
+        kernel,
+        in_specs=specs,
+        out_specs=[whole()] * len(outs),
+        out_shape=outs,
+        input_output_aliases=aliases,
         scratch_shapes=[
             VMEM((2 * blocks, width), BF16),
             VMEM((rows, 2 * blocks), BF16),
             VMEM((rows, blocks), F32),
-            *sems,
+            pltpu.SemaphoreType.DMA((max(rows, 1 if following is None else following.shape[0]) // step,)),
         ],
         compiler_params=pltpu.CompilerParams(vmem_limit_bytes=MIB // 2 + 6 * LANES * rows),
         cost_estimate=pl.CostEstimate(flops=5 * 10**9, bytes_accessed=2 * rows * width, transcendentals=0),
-    )(code, scale_t)
+    )(*operands)
 
 
 def hidden_kernel(parts, groups, span, place, *refs):
@@ -335,16 +363,19 @@
     outgoing = pack(place, routes_t, tokens, parts)
     arrived = {d: to_expert(outgoing[d], d) for d in order}
 
-    w_gate = dequant(gate_code, gate_scale.T, 0)
-    w_up = dequant(up_code, up_scale.T, 0)
-    w_down = dequant(down_code, down_scale.T, 3)
-
-    def rows_of(chunk):
-        joined = join([arrived[d] for d in chunk])
+    step = math.gcd(math.gcd(gate_code.shape[0], down_code.shape[0]), 512)
+    early = max(1, down_code.shape[0] // step // 2)
+    (w_gate,) = dequant(gate_code, gate_scale.T, step)
+    w_up, begun = dequant(up_code, up_scale.T, step, following=down_code, early=early)
+    (w_down,) = dequant(down_code, down_scale.T, step, early=early, begun=begun)
+
+    def rows_of(chunks):
         xs = []
         for s in groups:
-            own = to_member(joined, s)
-            xs.append([to_part(own, (parts - p) % parts) for p in range(parts)])
+            for chunk in chunks if s else [sum(chunks, ())]:
+                own = join([arrived[d] for d in chunk]) if len(chunk) > 1 else arrived[chunk[0]]
+                own = to_member(own, s)
+                xs.append([to_part(own, (parts - p) % parts) for p in range(parts)])
         return xs
 
     def reduced(hs, sizes):
@@ -359,13 +390,10 @@
         return terms
 
     units = w_gate.shape[1]
-    far_hidden = hidden_of(place, rows_of(FAR), w_gate, w_up, (0, units))
+    far_hidden = hidden_of(place, rows_of([(d,) for d in FAR]), w_gate, w_up, (0, units))
     far_terms = reduced([far_hidden], [CAP * len(FAR)] * members)
-    near_rows = rows_of(NEAR)
-    half = units // 2
-    near_hidden = [
-        hidden_of(place, near_rows, w_gate, w_up, (0, half)), hidden_of(place, near_rows, w_gate, w_up, (half, units))
-    ]
+    near_rows = rows_of([NEAR])
+    near_hidden = hidden_of(place, near_rows, w_gate, w_up, (0, units))
     pieces = [[] for _ in range(EXPERTS)]
     for i, d in enumerate(FAR):
         start = i * CAP
@@ -376,7 +404,7 @@
             starts.append(0)
         (total,) = add_rows(terms, [starts])
         pieces[d].append(to_expert(total, d))
-    (near_terms,) = reduced(near_hidden, [CAP * len(NEAR) * members])
+    (near_terms,) = reduced([near_hidden], [CAP * len(NEAR) * members])
     slots = [(s, i) for s in groups for i in range(len(NEAR))]
     starts = [[(s * len(NEAR) + i) * CAP] * len(near_terms) for s, i in slots]
     for (s, i), total in zip(slots, add_rows(near_terms, starts)):

time: 71.8 us -> 65.2 us (0.908)
  waiting for transfers between devices: 14.8 us -> 10.4 us
  Pallas kernels: 36.1 us -> 32.6 us
  starting transfers between devices: 19.5 us -> 21.7 us
  local copies, waits for them, and re-layouts: 0.87 us -> 0.04 us
    ppermute x19 -> x21, waiting for transfers between devices: 14.8 us -> 10.4 us  [send(): return lax.ppermute(x, ('ep', 'tp'), pairs)]
    pallas_call x4, Pallas kernels: 15.3 us -> 12.6 us  [the longest x3 10.5 us: dequant(): pl.pallas_call(kernel, in_specs=specs, out_specs=[whole()] * len(outs), o...]
    ppermute x19 -> x21, starting transfers between devices: 19.5 us -> 21.7 us  [send(): return lax.ppermute(x, ('ep', 'tp'), pairs)]
    unnamed x20 -> x18, local copies, waits for them, and re-layouts: 0.87 us -> 0.04 us
    pallas_call x3 -> x2, Pallas kernels: 11 us -> 10.3 us  [hidden_of(): pl.pallas_call(functools.partial(hidden_kernel, parts, len(xs), span), in...]
  transfers between devices with their start and end apart: 19 -> 21, of which waited for: 7 -> 5; matrix products, arithmetic and copies ran while one was open for 0% -> 0% of each run, Pallas kernels for 44% -> 45%
where the time goes in v2:
time: 65.2 us; the launch traced here: 65.1 us
  Pallas kernels  32.6 us (50%)
  starting transfers between devices  21.7 us (33%)
  waiting for transfers between devices  10.4 us (16%)
    ppermute x21, starting transfers between devices, send(): return lax.ppermute(x, ('ep', 'tp'), pairs)  21.7 us
    pallas_call x3, Pallas kernels, dequant(): pl.pallas_call(kernel, in_specs=specs, out_specs=[whole()] * len(outs), o...  10.5 us
    ppermute x21, waiting for transfers between devices, send(): return lax.ppermute(x, ('ep', 'tp'), pairs)  10.4 us
    pallas_call x2, Pallas kernels, hidden_of(): pl.pallas_call(functools.partial(hidden_kernel, parts, len(xs), span), in...  10.3 us
    pallas_call x4, Pallas kernels, down(): pl.pallas_call(functools.partial(down_kernel, len(hs), shift, parts), in_...  7.12 us
    pallas_call x1, Pallas kernels, pack(): pl.pallas_call(pack_kernel, in_specs=[scalar(), in_hbm, in_hbm], out_spec...  2.09 us
    pallas_call x1, Pallas kernels, mix(): pl.pallas_call(functools.partial(mix_kernel, owners), in_specs=[whole()]...  1.42 us
  transfers between devices with their start and end apart: 21, of which 5 were waited for; matrix products, arithmetic and copies ran while one was open for 0% of the time, Pallas kernels for 45%

profile of v2, /device:TPU:0, one launch (start us, length us, event | category | flops | bytes accessed | tf_op | source)
XLA Modules:
  0.0 65.1 jit_solution(4395099298543293826)
XLA Ops:
  0.1 2.1 %pack.1 = (bf16[40,1536]{1,0:T(8,128)(2,1)S(1)}, bf16[40,1536]{1,0:T(8,128)(2,1)S(1)}, bf16[40,1536]{1,0:T(8,128)(2,1)S(1)}, bf16[40,1536]{1,0:T(8,128)(2,1)S(1)}) custom-call(s32[2]{0:T(128)S(1)} %pad_add_fusion.place, s32[2,64]{1,0:T(2,128)} %bitcast.12, bf16[64,3072]{1,0:T(8,128)(2,1)} %tokens_hbm.1), custom_call_target="tpu_custom_call" | custom-call | flops 6000000000 | tf_op jit(solution)/shard_map/pack/pallas_call | solution.py:70
  2.2 3.1 %collective-permute-start = (bf16[40,1536]{1,0:T(8,128)(2,1)S(1)}, bf16[40,1536]{1,0:T(8,128)(2,1)S(1)}, u32[]{:S(2)}, u32[]{:S(2)}) collective-permute-start(bf16[40,1536]{1,0:T(8,128)(2,1)S(1)} %get-tuple-element.29), channel_id=1, source_target_pairs={{0,4},{1,5},{2,6},{3,7},{4,0},{5,1},{6,2},{7,3},{8,12},{9,13},{10,... | collective-permute-start | bytes 368648 | tf_op jit(solution)/shard_map/ppermute | solution.py:347
  5.3 2.5 %collective-permute-start.8 = (bf16[40,1536]{1,0:T(8,128)(2,1)S(1)}, bf16[40,1536]{1,0:T(8,128)(2,1)S(1)}, u32[]{:S(2)}, u32[]{:S(2)}) collective-permute-start(bf16[40,1536]{1,0:T(8,128)(2,1)S(1)} %get-tuple-element.37), channel_id=1, source_target_pairs={{0,12},{1,13},{2,14},{3,15},{4,8},{5,9},{6,10},{7,11},{8,4},{9,5},... | collective-permute-start | bytes 368648 | tf_op jit(solution)/shard_map/ppermute | solution.py:347
  7.9 3.3 %shard_map.92.refs_4_.refs_6_ = bf16[3072,2048]{1,0:T(8,128)(2,1)S(1)} custom-call(bf16[3072,2048]{1,0:T(8,128)(2,1)S(1)} %copy-done, f32[16,3072]{1,0:T(8,128)S(1)} %bitcast.9), custom_call_target="tpu_custom_call" | custom-call | flops 5000000000 | bytes 12582912 | tf_op jit(solution)/shard_map/pallas_call | solution.py:145
  11.3 1.6 %collective-permute-start.2 = (bf16[80,1536]{1,0:T(8,128)(2,1)S(1)}, bf16[80,1536]{1,0:T(8,128)(2,1)S(1)}, u32[]{:S(2)}, u32[]{:S(2)}) collective-permute-start(bf16[80,1536]{1,0:T(8,128)(2,1)S(1)} %shard_map.91.refs_0_), channel_id=1, source_target_pairs={{0,2},{1,3},{2,0},{3,1},{4,6},{5,7},{6,4},{7,5},{8,10},{9,11},{10,... | collective-permute-start | bytes 737288 | tf_op jit(solution)/shard_map/ppermute | solution.py:347
  12.9 3.4 %shard_map.93 = (bf16[3072,2048]{1,0:T(8,128)(2,1)S(1)}, bf16[2048,3072]{1,0:T(8,128)(2,1)S(1)}) custom-call(bf16[3072,2048]{1,0:T(8,128)(2,1)S(1)} %bitcast.8, f32[16,3072]{1,0:T(8,128)S(1)} %bitcast.10, bf16[2048,3072]{1,0:T(8,128)(2,1)} %code.5), custom_call_target="tpu_custom_call" | custom-call | flops 5000000000 | bytes 12582912 | tf_op jit(solution)/shard_map/pallas_call | solution.py:145
  16.4 0.6 collective-permute-start.11
  17.0 1.9 %collective-permute-done.9.refs_1_ = bf16[40,1536]{1,0:T(8,128)(2,1)S(1)} collective-permute-done((bf16[40,1536]{1,0:T(8,128)(2,1)S(1)}, bf16[40,1536]{1,0:T(8,128)(2,1)S(1)}, u32[]{:S(2)}, u32[]{:S(2)}) %collective-permute-start.9) | collective-permute-done | bytes 122912 | tf_op jit(solution)/shard_map/ppermute | solution.py:347
  18.8 1.5 %collective-permute-start.13 = (bf16[40,1536]{1,0:T(8,128)(2,1)S(1)}, bf16[40,1536]{1,0:T(8,128)(2,1)S(1)}, u32[]{:S(2)}, u32[]{:S(2)}) collective-permute-start(bf16[40,1536]{1,0:T(8,128)(2,1)S(1)} %collective-permute-done.9.refs_1_), channel_id=1, source_target_pairs={{0,2},{1,3},{2,0},{3,1},{4,6},{5,7},{6,4},{7,5},{8,10},{9,11},{10,... | collective-permute-start | bytes 368648 | tf_op jit(solution)/shard_map/ppermute | solution.py:347
  20.4 3.8 %shard_map.95.refs_1_ = bf16[2048,3072]{1,0:T(8,128)(2,1)S(1)} custom-call(bf16[2048,3072]{1,0:T(8,128)(2,1)} %code.5, f32[24,2048]{1,0:T(8,128)S(1)} %bitcast.11, bf16[2048,3072]{1,0:T(8,128)(2,1)S(1)} %get-tuple-element.32.refs_0_), custom_call_target="tpu_custom_call", output_to_operand_aliasing={{}: (2, {})} | custom-call | flops 5000000000 | bytes 12582912 | tf_op jit(solution)/shard_map/pallas_call | solution.py:145
  24.1 0.6 collective-permute-start.10
  24.8 0.4 collective-permute-start.14
  25.2 5.2 %shard_map.94.refs_0_ = bf16[160,2048]{1,0:T(8,128)(2,1)S(1)} custom-call(s32[2]{0:T(128)S(1)} %pad_add_fusion.place, bf16[80,1536]{1,0:T(8,128)(2,1)S(1)} %shard_map.91.refs_0_, bf16[80,1536]{1,0:T(8,128)(2,1)S(1)} %collective-permute-done.1.refs_1_, bf16[80,1536]{1,0:T(8,128)(2,1)S(1)} %collective-permute-done.2.refs_2_, ...), custom_call_target="tpu_custom_call" | custom-call | flops 4026531840 | tf_op jit(solution)/shard_map/pallas_call | solution.py:191
  30.5 1.8 %shard_map.96 = bf16[160,1536]{1,0:T(8,128)(2,1)S(1)} custom-call(s32[2]{0:T(128)S(1)} %pad_add_fusion.place, bf16[160,2048]{1,0:T(8,128)(2,1)S(1)} %shard_map.94.refs_0_, bf16[2048,3072]{1,0:T(8,128)(2,1)S(1)} %shard_map.95.refs_1_), custom_call_target="tpu_custom_call" | custom-call | flops 1006632960 | tf_op jit(solution)/shard_map/pallas_call | solution.py:226
  32.4 5.1 %shard_map.100.refs_0_ = bf16[160,2048]{1,0:T(8,128)(2,1)S(1)} custom-call(s32[2]{0:T(128)S(1)} %pad_add_fusion.place, bf16[80,1536]{1,0:T(8,128)(2,1)S(1)} %shard_map.99.refs_0_, bf16[80,1536]{1,0:T(8,128)(2,1)S(1)} %collective-permute-done.10.refs_1_, bf16[40,1536]{1,0:T(8,128)(2,1)S(1)} %collective-permute-done.11.refs_2_, ...), custom_call_target="tpu_custom_call" | custom-call | flops 4026531840 | tf_op jit(solution)/shard_map/pallas_call | solution.py:191
  37.5 1.8 %shard_map.101 = (bf16[80,1536]{1,0:T(8,128)(2,1)S(1)}, bf16[80,1536]{1,0:T(8,128)(2,1)S(1)}) custom-call(s32[2]{0:T(128)S(1)} %pad_add_fusion.place, bf16[160,2048]{1,0:T(8,128)(2,1)S(1)} %shard_map.100.refs_0_, bf16[2048,3072]{1,0:T(8,128)(2,1)S(1)} %shard_map.95.refs_1_), custom_call_target="tpu_custom_call" | custom-call | flops 1006632960 | tf_op jit(solution)/shard_map/pallas_call | solution.py:226
  39.3 0.5 collective-permute-start.16
  39.9 1.8 %shard_map.102 = (f32[80,1536]{1,0:T(8,128)S(1)}, f32[80,1536]{1,0:T(8,128)S(1)}) custom-call(s32[2]{0:T(128)S(1)} %pad_add_fusion.place, bf16[160,2048]{1,0:T(8,128)(2,1)S(1)} %shard_map.100.refs_0_, bf16[2048,3072]{1,0:T(8,128)(2,1)S(1)} %shard_map.95.refs_1_), custom_call_target="tpu_custom_call" | custom-call | flops 1006632960 | tf_op jit(solution)/shard_map/pallas_call | solution.py:226
  41.7 0.6 collective-permute-start.17
  42.3 1.6 %collective-permute-start.19 = (bf16[40,1536]{1,0:T(8,128)(2,1)S(1)}, bf16[40,1536]{1,0:T(8,128)(2,1)S(1)}, u32[]{:S(2)}, u32[]{:S(2)}) collective-permute-start(bf16[40,1536]{1,0:T(8,128)(2,1)S(1)} %shard_map.105), channel_id=1, source_target_pairs={{0,2},{1,3},{2,0},{3,1},{4,6},{5,7},{6,4},{7,5},{8,10},{9,11},{10,... | collective-permute-start | bytes 368648 | tf_op jit(solution)/shard_map/ppermute | solution.py:347
  43.9 1.8 %shard_map.97.refs_1_ = f32[160,1536]{1,0:T(8,128)S(1)} custom-call(s32[2]{0:T(128)S(1)} %pad_add_fusion.place, bf16[160,2048]{1,0:T(8,128)(2,1)S(1)} %shard_map.94.refs_0_, bf16[2048,3072]{1,0:T(8,128)(2,1)S(1)} %shard_map.95.refs_1_), custom_call_target="tpu_custom_call" | custom-call | flops 1006632960 | tf_op jit(solution)/shard_map/pallas_call | solution.py:226
  45.7 2.3 %collective-permute-done.17.refs_2_ = bf16[40,1536]{1,0:T(8,128)(2,1)S(1)} collective-permute-done((bf16[40,1536]{1,0:T(8,128)(2,1)S(1)}, bf16[40,1536]{1,0:T(8,128)(2,1)S(1)}, u32[]{:S(2)}, u32[]{:S(2)}) %collective-permute-start.17) | collective-permute-done | bytes 122912 | tf_op jit(solution)/shard_map/ppermute | solution.py:347
  48.0 2.8 %collective-permute-start.18 = (bf16[40,1536]{1,0:T(8,128)(2,1)S(1)}, bf16[40,1536]{1,0:T(8,128)(2,1)S(1)}, u32[]{:S(2)}, u32[]{:S(2)}) collective-permute-start(bf16[40,1536]{1,0:T(8,128)(2,1)S(1)} %shard_map.104), channel_id=1, source_target_pairs={{0,8},{1,9},{2,10},{3,11},{4,12},{5,13},{6,14},{7,15},{8,0},{9,1},... | collective-permute-start | bytes 368648 | tf_op jit(solution)/shard_map/ppermute | solution.py:347
  50.9 1.9 %collective-permute-start.20 = (bf16[40,1536]{1,0:T(8,128)(2,1)S(1)}, bf16[40,1536]{1,0:T(8,128)(2,1)S(1)}, u32[]{:S(2)}, u32[]{:S(2)}) collective-permute-start(bf16[40,1536]{1,0:T(8,128)(2,1)S(1)} %shard_map.106), channel_id=1, source_target_pairs={{0,12},{1,13},{2,14},{3,15},{4,8},{5,9},{6,10},{7,11},{8,4},{9,5},... | collective-permute-start | bytes 368648 | tf_op jit(solution)/shard_map/ppermute | solution.py:347
  52.9 0.6 collective-permute-start.5
  53.5 0.3 collective-permute-start.6
  53.8 2.6 %collective-permute-start.7 = (bf16[40,1536]{1,0:T(8,128)(2,1)S(1)}, bf16[40,1536]{1,0:T(8,128)(2,1)S(1)}, u32[]{:S(2)}, u32[]{:S(2)}) collective-permute-start(bf16[40,1536]{1,0:T(8,128)(2,1)S(1)} %get-tuple-element.36), channel_id=1, source_target_pairs={{0,6},{1,7},{2,4},{3,5},{4,2},{5,3},{6,0},{7,1},{8,14},{9,15},{10,... | collective-permute-start | bytes 368648 | tf_op jit(solution)/shard_map/ppermute | solution.py:347
  56.5 1.0 %plan.1 = (bf16[128,40]{1,0:T(8,128)(2,1)S(1)}, bf16[128,40]{1,0:T(8,128)(2,1)S(1)}, bf16[128,40]{1,0:T(8,128)(2,1)S(1)}, bf16[128,40]{1,0:T(8,128)(2,1)S(1)}, f32[64,2]{1,0:T(8,128)S(1)}) custom-call(s32[2]{0:T(128)S(1)} %pad_add_fusion.place, s32[2,64]{1,0:T(2,128)S(1)} %bitcast.13, f32[2,64]{1,0:T(2,128)S(1)} %bitcast.14), custom_call_target="tpu_custom_call" | custom-call | tf_op jit(solution)/shard_map/plan/pallas_call | solution.py:293
  57.4 1.7 %collective-permute-done.18.refs_9_ = bf16[40,1536]{1,0:T(8,128)(2,1)S(1)} collective-permute-done((bf16[40,1536]{1,0:T(8,128)(2,1)S(1)}, bf16[40,1536]{1,0:T(8,128)(2,1)S(1)}, u32[]{:S(2)}, u32[]{:S(2)}) %collective-permute-start.18) | collective-permute-done | bytes 122912 | tf_op jit(solution)/shard_map/ppermute | solution.py:347
  59.1 2.1 %collective-permute-done.6.refs_7_ = bf16[40,1536]{1,0:T(8,128)(2,1)S(1)} collective-permute-done((bf16[40,1536]{1,0:T(8,128)(2,1)S(1)}, bf16[40,1536]{1,0:T(8,128)(2,1)S(1)}, u32[]{:S(2)}, u32[]{:S(2)}) %collective-permute-start.6) | collective-permute-done | bytes 122912 | tf_op jit(solution)/shard_map/ppermute | solution.py:347
  61.2 2.4 %collective-permute-done.7.refs_8_ = bf16[40,1536]{1,0:T(8,128)(2,1)S(1)} collective-permute-done((bf16[40,1536]{1,0:T(8,128)(2,1)S(1)}, bf16[40,1536]{1,0:T(8,128)(2,1)S(1)}, u32[]{:S(2)}, u32[]{:S(2)}) %collective-permute-start.7) | collective-permute-done | bytes 122912 | tf_op jit(solution)/shard_map/ppermute | solution.py:347
  63.6 1.4 %mix.1 = bf16[64,1536]{1,0:T(8,128)(2,1)} custom-call(f32[64,2]{1,0:T(8,128)S(1)} %get-tuple-element.24.refs_0_, bf16[128,40]{1,0:T(8,128)(2,1)S(1)} %get-tuple-element.25.refs_1_, bf16[128,40]{1,0:T(8,128)(2,1)S(1)} %get-tuple-element.26.refs_2_, bf16[128,40]{1,0:T(8,128)(2,1)S(1)} %get-tuple-element.27.refs_3_, ...), custom_call_target="tpu_custom_call" | custom-call | tf_op jit(solution)/shard_map/mix/pallas_call | solution.py:323
  (49 shorter events, 1.0 us)
Async XLA Ops:
  0.0 7.9 %copy-start.1 = (f32[3072,16]{0,1:T(8,128)S(1)}, f32[3072,16]{0,1:T(8,128)}, u32[]{:S(2)}) copy-start(f32[3072,16]{0,1:T(8,128)} %param.13) | copy-start | bytes 589828
  0.0 7.9 %copy-start = (bf16[3072,2048]{1,0:T(8,128)(2,1)S(1)}, bf16[3072,2048]{1,0:T(8,128)(2,1)}, u32[]{:S(2)}) copy-start(bf16[3072,2048]{1,0:T(8,128)(2,1)} %code.3) | copy-start | bytes 37748740
  0.1 12.8 %slice-start = ((s8[12582912]{0:T(1024)(128)(4,1)}), s8[4194304]{0:T(1024)(128)(4,1)S(1)}, s32[]{:S(2)}) async-start(s8[12582912]{0:T(1024)(128)(4,1)} %bitcast.7), calls=%async_computation | async-start | bytes 8388608
  0.1 12.8 %slice-start.1 = ((s8[12582912]{0:T(1024)(128)(4,1)}), s8[4194304]{0:T(1024)(128)(4,1)S(1)}, s32[]{:S(2)}) async-start(s8[12582912]{0:T(1024)(128)(4,1)} %bitcast.7), calls=%async_computation.1 | async-start | bytes 8388608
  2.2 9.1 %collective-permute-start = (bf16[40,1536]{1,0:T(8,128)(2,1)S(1)}, bf16[40,1536]{1,0:T(8,128)(2,1)S(1)}, u32[]{:S(2)}, u32[]{:S(2)}) collective-permute-start(bf16[40,1536]{1,0:T(8,128)(2,1)S(1)} %get-tuple-element.29), channel_id=1, source_target_pairs={{0,4},{1,5},{2,6},{3,7},{4,0},{5,1},{6,2},{7,3},{8,12},{9,13},{10,... | collective-permute-start | bytes 368648 | tf_op jit(solution)/shard_map/ppermute | solution.py:347
  5.3 11.1 %collective-permute-start.8 = (bf16[40,1536]{1,0:T(8,128)(2,1)S(1)}, bf16[40,1536]{1,0:T(8,128)(2,1)S(1)}, u32[]{:S(2)}, u32[]{:S(2)}) collective-permute-start(bf16[40,1536]{1,0:T(8,128)(2,1)S(1)} %get-tuple-element.37), channel_id=1, source_target_pairs={{0,12},{1,13},{2,14},{3,15},{4,8},{5,9},{6,10},{7,11},{8,4},{9,5},... | collective-permute-start | bytes 368648 | tf_op jit(solution)/shard_map/ppermute | solution.py:347
  7.8 11.1 %collective-permute-start.9 = (bf16[40,1536]{1,0:T(8,128)(2,1)S(1)}, bf16[40,1536]{1,0:T(8,128)(2,1)S(1)}, u32[]{:S(2)}, u32[]{:S(2)}) collective-permute-start(bf16[40,1536]{1,0:T(8,128)(2,1)S(1)} %get-tuple-element.38), channel_id=1, source_target_pairs={{0,8},{1,9},{2,10},{3,11},{4,12},{5,13},{6,14},{7,15},{8,0},{9,1},... | collective-permute-start | bytes 368648 | tf_op jit(solution)/shard_map/ppermute | solution.py:347
  7.9 5.0 %slice-start.2 = ((s8[12582912]{0:T(1024)(128)(4,1)}), s8[4194304]{0:T(1024)(128)(4,1)S(1)}, s32[]{:S(2)}) async-start(s8[12582912]{0:T(1024)(128)(4,1)} %bitcast.7), calls=%async_computation.2 | async-start | bytes 8388608
  7.9 5.0 %copy-start.2 = (f32[3072,16]{0,1:T(8,128)S(1)}, f32[3072,16]{0,1:T(8,128)}, u32[]{:S(2)}) copy-start(f32[3072,16]{0,1:T(8,128)} %param.15) | copy-start | bytes 589828
  11.3 9.1 %collective-permute-start.2 = (bf16[80,1536]{1,0:T(8,128)(2,1)S(1)}, bf16[80,1536]{1,0:T(8,128)(2,1)S(1)}, u32[]{:S(2)}, u32[]{:S(2)}) collective-permute-start(bf16[80,1536]{1,0:T(8,128)(2,1)S(1)} %shard_map.91.refs_0_), channel_id=1, source_target_pairs={{0,2},{1,3},{2,0},{3,1},{4,6},{5,7},{6,4},{7,5},{8,10},{9,11},{10,... | collective-permute-start | bytes 737288 | tf_op jit(solution)/shard_map/ppermute | solution.py:347
  12.9 7.5 %copy-start.3 = (f32[2048,24]{0,1:T(8,128)S(1)}, f32[2048,24]{0,1:T(8,128)}, u32[]{:S(2)}) copy-start(f32[2048,24]{0,1:T(8,128)} %param.17) | copy-start | bytes 589828
  16.3 8.9 %collective-permute-start.1 = (bf16[80,1536]{1,0:T(8,128)(2,1)S(1)}, bf16[80,1536]{1,0:T(8,128)(2,1)S(1)}, u32[]{:S(2)}, u32[]{:S(2)}) collective-permute-start(bf16[80,1536]{1,0:T(8,128)(2,1)S(1)} %shard_map.91.refs_0_), channel_id=1, source_target_pairs={{0,1},{1,0},{2,3},{3,2},{4,5},{5,4},{6,7},{7,6},{8,9},{9,8},{10,11... | collective-permute-start | bytes 737288 | tf_op jit(solution)/shard_map/ppermute | solution.py:347
  16.4 8.3 %collective-permute-start.11 = (bf16[40,1536]{1,0:T(8,128)(2,1)S(1)}, bf16[40,1536]{1,0:T(8,128)(2,1)S(1)}, u32[]{:S(2)}, u32[]{:S(2)}) collective-permute-start(bf16[40,1536]{1,0:T(8,128)(2,1)S(1)} %collective-permute-done.8.refs_0_), channel_id=1, source_target_pairs={{0,2},{1,3},{2,0},{3,1},{4,6},{5,7},{6,4},{7,5},{8,10},{9,11},{10,... | collective-permute-start | bytes 368648 | tf_op jit(solution)/shard_map/ppermute | solution.py:347
  18.8 6.0 %collective-permute-start.13 = (bf16[40,1536]{1,0:T(8,128)(2,1)S(1)}, bf16[40,1536]{1,0:T(8,128)(2,1)S(1)}, u32[]{:S(2)}, u32[]{:S(2)}) collective-permute-start(bf16[40,1536]{1,0:T(8,128)(2,1)S(1)} %collective-permute-done.9.refs_1_), channel_id=1, source_target_pairs={{0,2},{1,3},{2,0},{3,1},{4,6},{5,7},{6,4},{7,5},{8,10},{9,11},{10,... | collective-permute-start | bytes 368648 | tf_op jit(solution)/shard_map/ppermute | solution.py:347
  20.3 4.9 %collective-permute-start.3 = (bf16[80,1536]{1,0:T(8,128)(2,1)S(1)}, bf16[80,1536]{1,0:T(8,128)(2,1)S(1)}, u32[]{:S(2)}, u32[]{:S(2)}) collective-permute-start(bf16[80,1536]{1,0:T(8,128)(2,1)S(1)} %collective-permute-done.2.refs_2_), channel_id=1, source_target_pairs={{0,1},{1,0},{2,3},{3,2},{4,5},{5,4},{6,7},{7,6},{8,9},{9,8},{10,11... | collective-permute-start | bytes 737288 | tf_op jit(solution)/shard_map/ppermute | solution.py:347
  24.1 8.3 %collective-permute-start.10 = (bf16[80,1536]{1,0:T(8,128)(2,1)S(1)}, bf16[80,1536]{1,0:T(8,128)(2,1)S(1)}, u32[]{:S(2)}, u32[]{:S(2)}) collective-permute-start(bf16[80,1536]{1,0:T(8,128)(2,1)S(1)} %shard_map.99.refs_0_), channel_id=1, source_target_pairs={{0,1},{1,0},{2,3},{3,2},{4,5},{5,4},{6,7},{7,6},{8,9},{9,8},{10,11... | collective-permute-start | bytes 737288 | tf_op jit(solution)/shard_map/ppermute | solution.py:347
  24.7 7.7 %collective-permute-start.12 = (bf16[40,1536]{1,0:T(8,128)(2,1)S(1)}, bf16[40,1536]{1,0:T(8,128)(2,1)S(1)}, u32[]{:S(2)}, u32[]{:S(2)}) collective-permute-start(bf16[40,1536]{1,0:T(8,128)(2,1)S(1)} %collective-permute-done.11.refs_2_), channel_id=1, source_target_pairs={{0,1},{1,0},{2,3},{3,2},{4,5},{5,4},{6,7},{7,6},{8,9},{9,8},{10,11... | collective-permute-start | bytes 368648 | tf_op jit(solution)/shard_map/ppermute | solution.py:347
  24.8 7.6 %collective-permute-start.14 = (bf16[40,1536]{1,0:T(8,128)(2,1)S(1)}, bf16[40,1536]{1,0:T(8,128)(2,1)S(1)}, u32[]{:S(2)}, u32[]{:S(2)}) collective-permute-start(bf16[40,1536]{1,0:T(8,128)(2,1)S(1)} %collective-permute-done.13.refs_4_), channel_id=1, source_target_pairs={{0,1},{1,0},{2,3},{3,2},{4,5},{5,4},{6,7},{7,6},{8,9},{9,8},{10,11... | collective-permute-start | bytes 368648 | tf_op jit(solution)/shard_map/ppermute | solution.py:347
  32.3 20.5 %collective-permute-start.4 = (bf16[160,1536]{1,0:T(8,128)(2,1)S(1)}, bf16[160,1536]{1,0:T(8,128)(2,1)S(1)}, u32[]{:S(2)}, u32[]{:S(2)}) collective-permute-start(bf16[160,1536]{1,0:T(8,128)(2,1)S(1)} %shard_map.96), channel_id=1, source_target_pairs={{0,1},{1,0},{2,3},{3,2},{4,5},{5,4},{6,7},{7,6},{8,9},{9,8},{10,11... | collective-permute-start | bytes 1474568 | tf_op jit(solution)/shard_map/ppermute | solution.py:347
  39.3 2.4 %collective-permute-start.16 = (bf16[80,1536]{1,0:T(8,128)(2,1)S(1)}, bf16[80,1536]{1,0:T(8,128)(2,1)S(1)}, u32[]{:S(2)}, u32[]{:S(2)}) collective-permute-start(bf16[80,1536]{1,0:T(8,128)(2,1)S(1)} %get-tuple-element.41), channel_id=1, source_target_pairs={{0,1},{1,0},{2,3},{3,2},{4,5},{5,4},{6,7},{7,6},{8,9},{9,8},{10,11... | collective-permute-start | bytes 737288 | tf_op jit(solution)/shard_map/ppermute | solution.py:347
  39.8 5.9 %collective-permute-start.15 = (bf16[80,1536]{1,0:T(8,128)(2,1)S(1)}, bf16[80,1536]{1,0:T(8,128)(2,1)S(1)}, u32[]{:S(2)}, u32[]{:S(2)}) collective-permute-start(bf16[80,1536]{1,0:T(8,128)(2,1)S(1)} %get-tuple-element.39), channel_id=1, source_target_pairs={{0,1},{1,0},{2,3},{3,2},{4,5},{5,4},{6,7},{7,6},{8,9},{9,8},{10,11... | collective-permute-start | bytes 737288 | tf_op jit(solution)/shard_map/ppermute | solution.py:347
  41.6 14.8 %copy-start.4 = (s32[64,2]{0,1:T(2,128)S(1)}, s32[64,2]{0,1:T(2,128)}, u32[]{:S(2)}) copy-start(s32[64,2]{0,1:T(2,128)} %param.10) | copy-start | bytes 1540
  41.7 14.8 %copy-start.5 = (f32[64,2]{0,1:T(2,128)S(1)}, f32[64,2]{0,1:T(2,128)}, u32[]{:S(2)}) copy-start(f32[64,2]{0,1:T(2,128)} %param.11) | copy-start | bytes 1540
  41.7 6.3 %collective-permute-start.17 = (bf16[40,1536]{1,0:T(8,128)(2,1)S(1)}, bf16[40,1536]{1,0:T(8,128)(2,1)S(1)}, u32[]{:S(2)}, u32[]{:S(2)}) collective-permute-start(bf16[40,1536]{1,0:T(8,128)(2,1)S(1)} %shard_map.103), channel_id=1, source_target_pairs={{0,2},{1,3},{2,0},{3,1},{4,6},{5,7},{6,4},{7,5},{8,10},{9,11},{10,... | collective-permute-start | bytes 368648 | tf_op jit(solution)/shard_map/ppermute | solution.py:347
  42.3 8.6 %collective-permute-start.19 = (bf16[40,1536]{1,0:T(8,128)(2,1)S(1)}, bf16[40,1536]{1,0:T(8,128)(2,1)S(1)}, u32[]{:S(2)}, u32[]{:S(2)}) collective-permute-start(bf16[40,1536]{1,0:T(8,128)(2,1)S(1)} %shard_map.105), channel_id=1, source_target_pairs={{0,2},{1,3},{2,0},{3,1},{4,6},{5,7},{6,4},{7,5},{8,10},{9,11},{10,... | collective-permute-start | bytes 368648 | tf_op jit(solution)/shard_map/ppermute | solution.py:347
  48.0 11.1 %collective-permute-start.18 = (bf16[40,1536]{1,0:T(8,128)(2,1)S(1)}, bf16[40,1536]{1,0:T(8,128)(2,1)S(1)}, u32[]{:S(2)}, u32[]{:S(2)}) collective-permute-start(bf16[40,1536]{1,0:T(8,128)(2,1)S(1)} %shard_map.104), channel_id=1, source_target_pairs={{0,8},{1,9},{2,10},{3,11},{4,12},{5,13},{6,14},{7,15},{8,0},{9,1},... | collective-permute-start | bytes 368648 | tf_op jit(solution)/shard_map/ppermute | solution.py:347
  50.9 8.2 %collective-permute-start.20 = (bf16[40,1536]{1,0:T(8,128)(2,1)S(1)}, bf16[40,1536]{1,0:T(8,128)(2,1)S(1)}, u32[]{:S(2)}, u32[]{:S(2)}) collective-permute-start(bf16[40,1536]{1,0:T(8,128)(2,1)S(1)} %shard_map.106), channel_id=1, source_target_pairs={{0,12},{1,13},{2,14},{3,15},{4,8},{5,9},{6,10},{7,11},{8,4},{9,5},... | collective-permute-start | bytes 368648 | tf_op jit(solution)/shard_map/ppermute | solution.py:347
  52.9 6.2 %collective-permute-start.5 = (bf16[40,1536]{1,0:T(8,128)(2,1)S(1)}, bf16[40,1536]{1,0:T(8,128)(2,1)S(1)}, u32[]{:S(2)}, u32[]{:S(2)}) collective-permute-start(bf16[40,1536]{1,0:T(8,128)(2,1)S(1)} %get-tuple-element.34), channel_id=1, source_target_pairs={{0,2},{1,3},{2,0},{3,1},{4,6},{5,7},{6,4},{7,5},{8,10},{9,11},{10,... | collective-permute-start | bytes 368648 | tf_op jit(solution)/shard_map/ppermute | solution.py:347
  53.5 7.7 %collective-permute-start.6 = (bf16[40,1536]{1,0:T(8,128)(2,1)S(1)}, bf16[40,1536]{1,0:T(8,128)(2,1)S(1)}, u32[]{:S(2)}, u32[]{:S(2)}) collective-permute-start(bf16[40,1536]{1,0:T(8,128)(2,1)S(1)} %get-tuple-element.35), channel_id=1, source_target_pairs={{0,4},{1,5},{2,6},{3,7},{4,0},{5,1},{6,2},{7,3},{8,12},{9,13},{10,... | collective-permute-start | bytes 368648 | tf_op jit(solution)/shard_map/ppermute | solution.py:347
  53.8 9.8 %collective-permute-start.7 = (bf16[40,1536]{1,0:T(8,128)(2,1)S(1)}, bf16[40,1536]{1,0:T(8,128)(2,1)S(1)}, u32[]{:S(2)}, u32[]{:S(2)}) collective-permute-start(bf16[40,1536]{1,0:T(8,128)(2,1)S(1)} %get-tuple-element.36), channel_id=1, source_target_pairs={{0,6},{1,7},{2,4},{3,5},{4,2},{5,3},{6,0},{7,1},{8,14},{9,15},{10,... | collective-permute-start | bytes 368648 | tf_op jit(solution)/shard_map/ppermute | solution.py:347

commit v3 on v2

--- a/solution.py
+++ b/solution.py
@@ -159,12 +159,12 @@
     )(*operands)
 
 
-def hidden_kernel(parts, groups, span, place, *refs):
+def hidden_kernel(parts, groups, span, *refs):
     xs, (w_gate, w_up, out, staged) = refs[: groups * parts], refs[groups * parts :]
     part = xs[0].shape[1]
     low, high = span
     block = min(256, high - low)
-    at = [pl.ds(pl.multiple_of(lax.rem(place[1] + p, parts) * part, part), part) for p in range(parts)]
+    at = [pl.ds(pl.multiple_of(lax.rem(lax.axis_index("tp") + p, parts) * part, part), part) for p in range(parts)]
     row = 0
     for g in range(groups):
         for p in range(parts):
@@ -183,14 +183,14 @@
         out[:, n * block : (n + 1) * block] = (gate / (1.0 + jnp.exp(-gate)) * up).astype(BF16)
 
 
-def hidden_of(place, xs, w_gate, w_up, span):
+def hidden_of(xs, w_gate, w_up, span):
     parts = len(xs[0])
     flat = [x for group in xs for x in group]
     rows = sum(group[0].shape[0] for group in xs)
     depth, width = w_gate.shape[0], span[1] - span[0]
     return pl.pallas_call(
         functools.partial(hidden_kernel, parts, len(xs), span),
-        in_specs=[scalar()] + [whole()] * (len(flat) + 2),
+        in_specs=[whole()] * (len(flat) + 2),
         out_specs=whole(),
         out_shape=jax.ShapeDtypeStruct((rows, width), BF16),
         scratch_shapes=[VMEM((rows, w_gate.shape[0]), BF16)],
@@ -198,14 +198,14 @@
         cost_estimate=pl.CostEstimate(
             flops=4 * rows * w_gate.shape[0] * width, bytes_accessed=0, transcendentals=rows * width
         ),
-    )(place, *flat, w_gate, w_up)
-
-
-def down_kernel(count, shift, parts, place, *refs):
+    )(*flat, w_gate, w_up)
+
+
+def down_kernel(count, shift, parts, *refs):
     hs, w, outs = refs[:count], refs[count], refs[count + 1 :]
     part = outs[0].shape[1]
-    block = min(256, part)
-    base = lax.rem(place[1] + shift, parts) * part
+    block = math.gcd(part, 256)
+    base = lax.rem(lax.axis_index("tp") + shift, parts) * part
     for n in range(part // block):
         at = pl.ds(pl.multiple_of(base + n * block, block), block)
         total, low = None, 0
@@ -220,17 +220,17 @@
             row += size
 
 
-def down(place, hs, w, sizes, shift, parts, dtype):
+def down(hs, w, sizes, shift, parts, dtype):
     part = w.shape[1] // parts
     rows = sum(sizes)
     return pl.pallas_call(
         functools.partial(down_kernel, len(hs), shift, parts),
-        in_specs=[scalar()] + [whole()] * (len(hs) + 1),
+        in_specs=[whole()] * (len(hs) + 1),
         out_specs=[whole()] * len(sizes),
         out_shape=[jax.ShapeDtypeStruct((size, part), dtype) for size in sizes],
         compiler_params=pltpu.CompilerParams(vmem_limit_bytes=1 * MIB),
         cost_estimate=pl.CostEstimate(flops=2 * rows * w.shape[0] * part, bytes_accessed=0, transcendentals=0),
-    )(place, *hs, w)
+    )(*hs, w)
 
 
 def join_kernel(*refs):
@@ -272,9 +272,9 @@
     )(*terms)
 
 
-def plan_kernel(place, routes_ref, weight_ref, *refs):
+def plan_kernel(members, routes_ref, weight_ref, *refs):
     *picks, weights = refs
-    own = place[0]
+    own = lax.axis_index("ep") // members
     routes_t = routes_ref[...]
     count = routes_t.shape[1]
     weights[...] = weight_ref[...].T
@@ -288,46 +288,74 @@
         pick[...] = jnp.where(hit, 1.0, 0.0).T.astype(BF16)
 
 
-def plan(place, routes_t, weight_t):
+def plan(members, routes_t, weight_t):
     count = routes_t.shape[1]
     *picks, weights = pl.pallas_call(
-        plan_kernel,
-        in_specs=[scalar()] + [whole()] * 2,
+        functools.partial(plan_kernel, members),
+        in_specs=[whole()] * 2,
         out_specs=[whole()] * (EXPERTS + 1),
         out_shape=[jax.ShapeDtypeStruct((TOP * count, CAP), BF16)] * EXPERTS
         + [jax.ShapeDtypeStruct((count, TOP), F32)],
         compiler_params=pltpu.CompilerParams(vmem_limit_bytes=4 * MIB),
         name="plan",
-    )(place, routes_t, weight_t)
+    )(routes_t, weight_t)
     return picks, weights
 
 
-def mix_kernel(owners, *refs):
-    weights, *refs, out = refs
-    picks, pieces = refs[:EXPERTS], refs[EXPERTS:]
-    count = out.shape[0]
-    gathered = None
+def gather_kernel(owners, *refs):
+    picks, refs = refs[:EXPERTS], refs[EXPERTS:]
+    pieces, refs = refs[: len(owners)], refs[len(owners) :]
+    total = refs[0][...] if len(refs) == 2 else None
     for d, piece in zip(owners, pieces):
         got = jnp.dot(picks[d][...], piece[...], preferred_element_type=F32)
-        gathered = got if gathered is None else gathered + got
-    total = None
-    for k in range(TOP):
-        term = gathered[k * count : (k + 1) * count, :] * weights[:, k : k + 1]
-        total = term if total is None else total + term
-    out[...] = total.astype(BF16)
-
-
-def mix(weights, picks, pieces):
-    owners = [d for d in range(EXPERTS) for _ in pieces[d]]
-    pieces = [x for d in range(EXPERTS) for x in pieces[d]]
+        total = got if total is None else total + got
+    refs[-1][...] = total
+
+
+def gather(picks, owners, pieces):
+    return pl.pallas_call(
+        functools.partial(gather_kernel, owners),
+        in_specs=[whole()] * (len(picks) + len(pieces)),
+        out_specs=whole(),
+        out_shape=jax.ShapeDtypeStruct((picks[0].shape[0], pieces[0].shape[1]), F32),
+        compiler_params=pltpu.CompilerParams(vmem_limit_bytes=2 * MIB),
+    )(*picks, *pieces)
+
+
+def mix_kernel(owners, early, weights, *refs):
+    picks, refs = refs[:EXPERTS], refs[EXPERTS:]
+    pieces, (out, staged, sems) = refs[: len(owners)], refs[len(owners) :]
+    count, width = out.shape
+    block = math.gcd(width, 512)
+    copies = []
+    for n in range(width // block):
+        cols = slice(n * block, (n + 1) * block)
+        gathered = early[:, cols]
+        for d, piece in zip(owners, pieces):
+            gathered = gathered + jnp.dot(picks[d][...], piece[:, cols], preferred_element_type=F32)
+        total = None
+        for k in range(TOP):
+            term = gathered[k * count : (k + 1) * count, :] * weights[:, k : k + 1]
+            total = term if total is None else total + term
+        staged[:, cols] = total.astype(BF16)
+        at = pl.ds(n * block, block)
+        copies.append(pltpu.make_async_copy(staged.at[:, at], out.at[:, at], sems.at[n]))
+        copies[-1].start()
+    for copy in copies:
+        copy.wait()
+
+
+def mix(weights, picks, early, owners, pieces):
+    count, width = weights.shape[0], early.shape[1]
     return pl.pallas_call(
         functools.partial(mix_kernel, owners),
-        in_specs=[whole()] * (1 + len(picks) + len(pieces)),
-        out_specs=whole(),
-        out_shape=jax.ShapeDtypeStruct((weights.shape[0], pieces[0].shape[1]), BF16),
+        in_specs=[whole()] * (2 + len(picks) + len(pieces)),
+        out_specs=pl.BlockSpec(memory_space=pltpu.HBM),
+        out_shape=jax.ShapeDtypeStruct((count, width), BF16),
+        scratch_shapes=[VMEM((count, width), BF16), pltpu.SemaphoreType.DMA((width // math.gcd(width, 512),))],
         compiler_params=pltpu.CompilerParams(vmem_limit_bytes=2 * MIB),
         name="mix",
-    )(weights, *picks, *pieces)
+    )(early, weights, *picks, *pieces)
 
 
 FAR, NEAR = (3, 2), (1, 0)
@@ -381,19 +409,19 @@
     def reduced(hs, sizes):
         terms = [[] for _ in sizes]
         for p in range(1, parts):
-            partial = down(place, hs, w_down, sizes, p, parts, BF16)
+            partial = down(hs, w_down, sizes, p, parts, BF16)
             for k in reversed(range(len(sizes))):
                 terms[k].append(to_part(partial[k], p))
-        own = down(place, hs, w_down, sizes, 0, parts, F32)
+        own = down(hs, w_down, sizes, 0, parts, F32)
         for k in range(len(sizes)):
             terms[k].append(own[k])
         return terms
 
     units = w_gate.shape[1]
-    far_hidden = hidden_of(place, rows_of([(d,) for d in FAR]), w_gate, w_up, (0, units))
+    far_hidden = hidden_of(rows_of([(d,) for d in FAR]), w_gate, w_up, (0, units))
     far_terms = reduced([far_hidden], [CAP * len(FAR)] * members)
     near_rows = rows_of([NEAR])
-    near_hidden = hidden_of(place, near_rows, w_gate, w_up, (0, units))
+    near_hidden = hidden_of(near_rows, w_gate, w_up, (0, units))
     pieces = [[] for _ in range(EXPERTS)]
     for i, d in enumerate(FAR):
         start = i * CAP
@@ -412,8 +440,11 @@
         if s or d:
             total = send(total, lambda e, m, t, d=d, s=s: (e ^ d, (m + members - s) % members, t))
         pieces[d].append(total)
-    picks, weights = plan(place, routes_t, weight_t)
-    return mix(weights, picks, pieces)
+    picks, weights = plan(members, routes_t, weight_t)
+    owners = [d for d in range(EXPERTS) for _ in pieces[d][:1]]
+    early = gather(picks, owners, [pieces[d][0] for d in owners])
+    owners = [d for d in range(EXPERTS) for _ in pieces[d][1:]]
+    return mix(weights, picks, early, owners, [x for d in range(EXPERTS) for x in pieces[d][1:]])
 
 
 def solution(mesh):

time: 65.2 us -> 61.1 us (0.937)
  Pallas kernels: 32.6 us -> 28.6 us
    pallas_call x4, Pallas kernels: 7.12 us -> 4.96 us  [down(): pl.pallas_call(functools.partial(down_kernel, len(hs), shift, parts), in_...]
    pallas_call x2, Pallas kernels: 10.3 us -> 8.82 us  [hidden_of(): pl.pallas_call(functools.partial(hidden_kernel, parts, len(xs), span), in...]
  transfers between devices with their start and end apart: 21 -> 21, of which waited for: 5 -> 6; matrix products, arithmetic and copies ran while one was open for 0% -> 0% of each run, Pallas kernels for 45% -> 42%
where the time goes in v3:
time: 61.1 us; the launch traced here: 60.9 us
  Pallas kernels  28.6 us (47%)
  starting transfers between devices  21.7 us (36%)
  waiting for transfers between devices  10.2 us (17%)
    ppermute x21, starting transfers between devices, send(): return lax.ppermute(x, ('ep', 'tp'), pairs)  21.7 us
    pallas_call x3, Pallas kernels, dequant(): pl.pallas_call(kernel, in_specs=specs, out_specs=[whole()] * len(outs), o...  10.5 us
    ppermute x21, waiting for transfers between devices, send(): return lax.ppermute(x, ('ep', 'tp'), pairs)  10.2 us
    pallas_call x2, Pallas kernels, hidden_of(): pl.pallas_call(functools.partial(hidden_kernel, parts, len(xs), span), in...  8.82 us
    pallas_call x4, Pallas kernels, down(): pl.pallas_call(functools.partial(down_kernel, len(hs), shift, parts), in_...  4.96 us
    pallas_call x1, Pallas kernels, pack(): pl.pallas_call(pack_kernel, in_specs=[scalar(), in_hbm, in_hbm], out_spec...  2.09 us
  transfers between devices with their start and end apart: 21, of which 6 were waited for; matrix products, arithmetic and copies ran while one was open for 0% of the time, Pallas kernels for 42%

profile of v3, /device:TPU:0, one launch (start us, length us, event | category | flops | bytes accessed | tf_op | source)
XLA Modules:
  0.0 60.9 jit_solution(16692715642744256501)
XLA Ops:
  0.1 2.1 %pack.1 = (bf16[40,1536]{1,0:T(8,128)(2,1)S(1)}, bf16[40,1536]{1,0:T(8,128)(2,1)S(1)}, bf16[40,1536]{1,0:T(8,128)(2,1)S(1)}, bf16[40,1536]{1,0:T(8,128)(2,1)S(1)}) custom-call(s32[2]{0:T(128)S(1)} %pad_add_fusion.place, s32[2,64]{1,0:T(2,128)} %bitcast.12, bf16[64,3072]{1,0:T(8,128)(2,1)} %tokens_hbm.1), custom_call_target="tpu_custom_call" | custom-call | flops 6000000000 | tf_op jit(solution)/shard_map/pack/pallas_call | solution.py:70
  2.2 3.1 %collective-permute-start = (bf16[40,1536]{1,0:T(8,128)(2,1)S(1)}, bf16[40,1536]{1,0:T(8,128)(2,1)S(1)}, u32[]{:S(2)}, u32[]{:S(2)}) collective-permute-start(bf16[40,1536]{1,0:T(8,128)(2,1)S(1)} %get-tuple-element.28), channel_id=1, source_target_pairs={{0,4},{1,5},{2,6},{3,7},{4,0},{5,1},{6,2},{7,3},{8,12},{9,13},{10,... | collective-permute-start | bytes 368648 | tf_op jit(solution)/shard_map/ppermute | solution.py:375
  5.3 2.5 %collective-permute-start.6 = (bf16[40,1536]{1,0:T(8,128)(2,1)S(1)}, bf16[40,1536]{1,0:T(8,128)(2,1)S(1)}, u32[]{:S(2)}, u32[]{:S(2)}) collective-permute-start(bf16[40,1536]{1,0:T(8,128)(2,1)S(1)} %get-tuple-element.34), channel_id=1, source_target_pairs={{0,12},{1,13},{2,14},{3,15},{4,8},{5,9},{6,10},{7,11},{8,4},{9,5},... | collective-permute-start | bytes 368648 | tf_op jit(solution)/shard_map/ppermute | solution.py:375
  7.9 3.4 %shard_map.92.refs_4_.refs_6_ = bf16[3072,2048]{1,0:T(8,128)(2,1)S(1)} custom-call(bf16[3072,2048]{1,0:T(8,128)(2,1)S(1)} %copy-done, f32[16,3072]{1,0:T(8,128)S(1)} %bitcast.9), custom_call_target="tpu_custom_call" | custom-call | flops 5000000000 | bytes 12582912 | tf_op jit(solution)/shard_map/pallas_call | solution.py:145
  11.3 1.6 %collective-permute-start.2 = (bf16[80,1536]{1,0:T(8,128)(2,1)S(1)}, bf16[80,1536]{1,0:T(8,128)(2,1)S(1)}, u32[]{:S(2)}, u32[]{:S(2)}) collective-permute-start(bf16[80,1536]{1,0:T(8,128)(2,1)S(1)} %shard_map.91.refs_0_), channel_id=1, source_target_pairs={{0,2},{1,3},{2,0},{3,1},{4,6},{5,7},{6,4},{7,5},{8,10},{9,11},{10,... | collective-permute-start | bytes 737288 | tf_op jit(solution)/shard_map/ppermute | solution.py:375
  13.0 3.4 %shard_map.93 = (bf16[3072,2048]{1,0:T(8,128)(2,1)S(1)}, bf16[2048,3072]{1,0:T(8,128)(2,1)S(1)}) custom-call(bf16[3072,2048]{1,0:T(8,128)(2,1)S(1)} %bitcast.8, f32[16,3072]{1,0:T(8,128)S(1)} %bitcast.10, bf16[2048,3072]{1,0:T(8,128)(2,1)} %code.5), custom_call_target="tpu_custom_call" | custom-call | flops 5000000000 | bytes 12582912 | tf_op jit(solution)/shard_map/pallas_call | solution.py:145
  16.5 0.6 collective-permute-start.9
  17.0 1.8 %collective-permute-done.7.refs_1_ = bf16[40,1536]{1,0:T(8,128)(2,1)S(1)} collective-permute-done((bf16[40,1536]{1,0:T(8,128)(2,1)S(1)}, bf16[40,1536]{1,0:T(8,128)(2,1)S(1)}, u32[]{:S(2)}, u32[]{:S(2)}) %collective-permute-start.7) | collective-permute-done | bytes 122912 | tf_op jit(solution)/shard_map/ppermute | solution.py:375
  18.8 1.5 %collective-permute-start.11 = (bf16[40,1536]{1,0:T(8,128)(2,1)S(1)}, bf16[40,1536]{1,0:T(8,128)(2,1)S(1)}, u32[]{:S(2)}, u32[]{:S(2)}) collective-permute-start(bf16[40,1536]{1,0:T(8,128)(2,1)S(1)} %collective-permute-done.7.refs_1_), channel_id=1, source_target_pairs={{0,2},{1,3},{2,0},{3,1},{4,6},{5,7},{6,4},{7,5},{8,10},{9,11},{10,... | collective-permute-start | bytes 368648 | tf_op jit(solution)/shard_map/ppermute | solution.py:375
  20.4 3.7 %shard_map.95.refs_1_ = bf16[2048,3072]{1,0:T(8,128)(2,1)S(1)} custom-call(bf16[2048,3072]{1,0:T(8,128)(2,1)} %code.5, f32[24,2048]{1,0:T(8,128)S(1)} %bitcast.11, bf16[2048,3072]{1,0:T(8,128)(2,1)S(1)} %get-tuple-element.31.refs_0_), custom_call_target="tpu_custom_call", output_to_operand_aliasing={{}: (2, {})} | custom-call | flops 5000000000 | bytes 12582912 | tf_op jit(solution)/shard_map/pallas_call | solution.py:145
  24.1 0.6 collective-permute-start.8
  25.2 4.5 %shard_map.94.refs_0_ = bf16[160,2048]{1,0:T(8,128)(2,1)S(1)} custom-call(bf16[80,1536]{1,0:T(8,128)(2,1)S(1)} %shard_map.91.refs_0_, bf16[80,1536]{1,0:T(8,128)(2,1)S(1)} %collective-permute-done.1.refs_1_, bf16[80,1536]{1,0:T(8,128)(2,1)S(1)} %collective-permute-done.2.refs_2_, bf16[80,1536]{1,0:T(8,128)(2,1)S(1)} %collective-permute-done.3.refs_3_, ...), custom_call_target="tpu_custom_call" | custom-call | flops 4026531840 | tf_op jit(solution)/shard_map/pallas_call | solution.py:191
  29.7 1.3 %shard_map.96 = bf16[160,1536]{1,0:T(8,128)(2,1)S(1)} custom-call(bf16[160,2048]{1,0:T(8,128)(2,1)S(1)} %shard_map.94.refs_0_, bf16[2048,3072]{1,0:T(8,128)(2,1)S(1)} %shard_map.95.refs_1_), custom_call_target="tpu_custom_call" | custom-call | flops 1006632960 | tf_op jit(solution)/shard_map/pallas_call | solution.py:226
  31.2 4.3 %shard_map.100.refs_0_ = bf16[160,2048]{1,0:T(8,128)(2,1)S(1)} custom-call(bf16[80,1536]{1,0:T(8,128)(2,1)S(1)} %shard_map.99.refs_0_, bf16[80,1536]{1,0:T(8,128)(2,1)S(1)} %collective-permute-done.8.refs_1_, bf16[40,1536]{1,0:T(8,128)(2,1)S(1)} %collective-permute-done.9.refs_2_, bf16[40,1536]{1,0:T(8,128)(2,1)S(1)} %collective-permute-done.10.refs_3_, ...), custom_call_target="tpu_custom_call" | custom-call | flops 4026531840 | tf_op jit(solution)/shard_map/pallas_call | solution.py:191
  35.5 1.2 %shard_map.101 = (bf16[80,1536]{1,0:T(8,128)(2,1)S(1)}, bf16[80,1536]{1,0:T(8,128)(2,1)S(1)}) custom-call(bf16[160,2048]{1,0:T(8,128)(2,1)S(1)} %shard_map.100.refs_0_, bf16[2048,3072]{1,0:T(8,128)(2,1)S(1)} %shard_map.95.refs_1_), custom_call_target="tpu_custom_call" | custom-call | flops 1006632960 | tf_op jit(solution)/shard_map/pallas_call | solution.py:226
  36.7 0.5 collective-permute-start.14
  37.3 1.2 %shard_map.102 = (f32[80,1536]{1,0:T(8,128)S(1)}, f32[80,1536]{1,0:T(8,128)S(1)}) custom-call(bf16[160,2048]{1,0:T(8,128)(2,1)S(1)} %shard_map.100.refs_0_, bf16[2048,3072]{1,0:T(8,128)(2,1)S(1)} %shard_map.95.refs_1_), custom_call_target="tpu_custom_call" | custom-call | flops 1006632960 | tf_op jit(solution)/shard_map/pallas_call | solution.py:226
  38.6 0.6 collective-permute-start.15
  39.2 1.5 %collective-permute-start.17 = (bf16[40,1536]{1,0:T(8,128)(2,1)S(1)}, bf16[40,1536]{1,0:T(8,128)(2,1)S(1)}, u32[]{:S(2)}, u32[]{:S(2)}) collective-permute-start(bf16[40,1536]{1,0:T(8,128)(2,1)S(1)} %shard_map.105), channel_id=1, source_target_pairs={{0,2},{1,3},{2,0},{3,1},{4,6},{5,7},{6,4},{7,5},{8,10},{9,11},{10,... | collective-permute-start | bytes 368648 | tf_op jit(solution)/shard_map/ppermute | solution.py:375
  40.8 1.2 %shard_map.97.refs_1_ = f32[160,1536]{1,0:T(8,128)S(1)} custom-call(bf16[160,2048]{1,0:T(8,128)(2,1)S(1)} %shard_map.94.refs_0_, bf16[2048,3072]{1,0:T(8,128)(2,1)S(1)} %shard_map.95.refs_1_), custom_call_target="tpu_custom_call" | custom-call | flops 1006632960 | tf_op jit(solution)/shard_map/pallas_call | solution.py:226
  42.0 2.8 %collective-permute-done.15.refs_2_ = bf16[40,1536]{1,0:T(8,128)(2,1)S(1)} collective-permute-done((bf16[40,1536]{1,0:T(8,128)(2,1)S(1)}, bf16[40,1536]{1,0:T(8,128)(2,1)S(1)}, u32[]{:S(2)}, u32[]{:S(2)}) %collective-permute-start.15) | collective-permute-done | bytes 122912 | tf_op jit(solution)/shard_map/ppermute | solution.py:375
  44.9 2.9 %collective-permute-start.16 = (bf16[40,1536]{1,0:T(8,128)(2,1)S(1)}, bf16[40,1536]{1,0:T(8,128)(2,1)S(1)}, u32[]{:S(2)}, u32[]{:S(2)}) collective-permute-start(bf16[40,1536]{1,0:T(8,128)(2,1)S(1)} %shard_map.104), channel_id=1, source_target_pairs={{0,8},{1,9},{2,10},{3,11},{4,12},{5,13},{6,14},{7,15},{8,0},{9,1},... | collective-permute-start | bytes 368648 | tf_op jit(solution)/shard_map/ppermute | solution.py:375
  47.9 1.8 %collective-permute-start.18 = (bf16[40,1536]{1,0:T(8,128)(2,1)S(1)}, bf16[40,1536]{1,0:T(8,128)(2,1)S(1)}, u32[]{:S(2)}, u32[]{:S(2)}) collective-permute-start(bf16[40,1536]{1,0:T(8,128)(2,1)S(1)} %shard_map.106), channel_id=1, source_target_pairs={{0,12},{1,13},{2,14},{3,15},{4,8},{5,9},{6,10},{7,11},{8,4},{9,5},... | collective-permute-start | bytes 368648 | tf_op jit(solution)/shard_map/ppermute | solution.py:375
  49.8 0.5 collective-permute-start.5
  50.3 0.5 collective-permute-start.19
  50.8 2.5 %collective-permute-start.20 = (bf16[40,1536]{1,0:T(8,128)(2,1)S(1)}, bf16[40,1536]{1,0:T(8,128)(2,1)S(1)}, u32[]{:S(2)}, u32[]{:S(2)}) collective-permute-start(bf16[40,1536]{1,0:T(8,128)(2,1)S(1)} %get-tuple-element.42), channel_id=1, source_target_pairs={{0,6},{1,7},{2,4},{3,5},{4,2},{5,3},{6,0},{7,1},{8,14},{9,15},{10,... | collective-permute-start | bytes 368648 | tf_op jit(solution)/shard_map/ppermute | solution.py:375
  53.3 0.4 plan.1
  53.8 2.3 %collective-permute-done.16.refs_6_ = bf16[40,1536]{1,0:T(8,128)(2,1)S(1)} collective-permute-done((bf16[40,1536]{1,0:T(8,128)(2,1)S(1)}, bf16[40,1536]{1,0:T(8,128)(2,1)S(1)}, u32[]{:S(2)}, u32[]{:S(2)}) %collective-permute-start.16) | collective-permute-done | bytes 122912 | tf_op jit(solution)/shard_map/ppermute | solution.py:375
  56.1 2.0 %collective-permute-done.5.refs_5_ = bf16[40,1536]{1,0:T(8,128)(2,1)S(1)} collective-permute-done((bf16[40,1536]{1,0:T(8,128)(2,1)S(1)}, bf16[40,1536]{1,0:T(8,128)(2,1)S(1)}, u32[]{:S(2)}, u32[]{:S(2)}) %collective-permute-start.5) | collective-permute-done | bytes 122912 | tf_op jit(solution)/shard_map/ppermute | solution.py:375
  58.1 0.5 shard_map.107.early
  58.7 1.0 %collective-permute-done.20.refs_5_ = bf16[40,1536]{1,0:T(8,128)(2,1)S(1)} collective-permute-done((bf16[40,1536]{1,0:T(8,128)(2,1)S(1)}, bf16[40,1536]{1,0:T(8,128)(2,1)S(1)}, u32[]{:S(2)}, u32[]{:S(2)}) %collective-permute-start.20) | collective-permute-done | bytes 122912 | tf_op jit(solution)/shard_map/ppermute | solution.py:375
  59.7 1.0 %mix.1 = bf16[64,1536]{1,0:T(8,128)(2,1)} custom-call(f32[128,1536]{1,0:T(8,128)S(1)} %shard_map.107.early, f32[64,2]{1,0:T(8,128)S(1)} %get-tuple-element.40.weights, bf16[128,40]{1,0:T(8,128)(2,1)S(1)} %get-tuple-element.24.refs_0_, bf16[128,40]{1,0:T(8,128)(2,1)S(1)} %get-tuple-element.25.refs_1_, bf16[128,40]{1,0:T(8,128)(2,1)S(1)} %get-tuple-element.26.refs_2_, ...), custom_call_target="tpu_custom_call" | custom-call | tf_op jit(solution)/shard_map/mix/pallas_call | solution.py:350
  (50 shorter events, 1.4 us)
Async XLA Ops:
  0.0 7.9 %copy-start.1 = (f32[3072,16]{0,1:T(8,128)S(1)}, f32[3072,16]{0,1:T(8,128)}, u32[]{:S(2)}) copy-start(f32[3072,16]{0,1:T(8,128)} %param.13) | copy-start | bytes 589828
  0.0 7.9 %copy-start = (bf16[3072,2048]{1,0:T(8,128)(2,1)S(1)}, bf16[3072,2048]{1,0:T(8,128)(2,1)}, u32[]{:S(2)}) copy-start(bf16[3072,2048]{1,0:T(8,128)(2,1)} %code.3) | copy-start | bytes 37748740
  0.1 12.9 %slice-start = ((s8[12582912]{0:T(1024)(128)(4,1)}), s8[4194304]{0:T(1024)(128)(4,1)S(1)}, s32[]{:S(2)}) async-start(s8[12582912]{0:T(1024)(128)(4,1)} %bitcast.7), calls=%async_computation | async-start | bytes 8388608
  0.1 12.9 %slice-start.1 = ((s8[12582912]{0:T(1024)(128)(4,1)}), s8[4194304]{0:T(1024)(128)(4,1)S(1)}, s32[]{:S(2)}) async-start(s8[12582912]{0:T(1024)(128)(4,1)} %bitcast.7), calls=%async_computation.1 | async-start | bytes 8388608
  2.2 9.1 %collective-permute-start = (bf16[40,1536]{1,0:T(8,128)(2,1)S(1)}, bf16[40,1536]{1,0:T(8,128)(2,1)S(1)}, u32[]{:S(2)}, u32[]{:S(2)}) collective-permute-start(bf16[40,1536]{1,0:T(8,128)(2,1)S(1)} %get-tuple-element.28), channel_id=1, source_target_pairs={{0,4},{1,5},{2,6},{3,7},{4,0},{5,1},{6,2},{7,3},{8,12},{9,13},{10,... | collective-permute-start | bytes 368648 | tf_op jit(solution)/shard_map/ppermute | solution.py:375
  5.3 11.1 %collective-permute-start.6 = (bf16[40,1536]{1,0:T(8,128)(2,1)S(1)}, bf16[40,1536]{1,0:T(8,128)(2,1)S(1)}, u32[]{:S(2)}, u32[]{:S(2)}) collective-permute-start(bf16[40,1536]{1,0:T(8,128)(2,1)S(1)} %get-tuple-element.34), channel_id=1, source_target_pairs={{0,12},{1,13},{2,14},{3,15},{4,8},{5,9},{6,10},{7,11},{8,4},{9,5},... | collective-permute-start | bytes 368648 | tf_op jit(solution)/shard_map/ppermute | solution.py:375
  7.8 11.1 %collective-permute-start.7 = (bf16[40,1536]{1,0:T(8,128)(2,1)S(1)}, bf16[40,1536]{1,0:T(8,128)(2,1)S(1)}, u32[]{:S(2)}, u32[]{:S(2)}) collective-permute-start(bf16[40,1536]{1,0:T(8,128)(2,1)S(1)} %get-tuple-element.35), channel_id=1, source_target_pairs={{0,8},{1,9},{2,10},{3,11},{4,12},{5,13},{6,14},{7,15},{8,0},{9,1},... | collective-permute-start | bytes 368648 | tf_op jit(solution)/shard_map/ppermute | solution.py:375
  7.9 5.0 %slice-start.2 = ((s8[12582912]{0:T(1024)(128)(4,1)}), s8[4194304]{0:T(1024)(128)(4,1)S(1)}, s32[]{:S(2)}) async-start(s8[12582912]{0:T(1024)(128)(4,1)} %bitcast.7), calls=%async_computation.2 | async-start | bytes 8388608
  7.9 5.0 %copy-start.2 = (f32[3072,16]{0,1:T(8,128)S(1)}, f32[3072,16]{0,1:T(8,128)}, u32[]{:S(2)}) copy-start(f32[3072,16]{0,1:T(8,128)} %param.15) | copy-start | bytes 589828
  11.3 9.0 %collective-permute-start.2 = (bf16[80,1536]{1,0:T(8,128)(2,1)S(1)}, bf16[80,1536]{1,0:T(8,128)(2,1)S(1)}, u32[]{:S(2)}, u32[]{:S(2)}) collective-permute-start(bf16[80,1536]{1,0:T(8,128)(2,1)S(1)} %shard_map.91.refs_0_), channel_id=1, source_target_pairs={{0,2},{1,3},{2,0},{3,1},{4,6},{5,7},{6,4},{7,5},{8,10},{9,11},{10,... | collective-permute-start | bytes 737288 | tf_op jit(solution)/shard_map/ppermute | solution.py:375
  13.0 7.4 %copy-start.3 = (f32[2048,24]{0,1:T(8,128)S(1)}, f32[2048,24]{0,1:T(8,128)}, u32[]{:S(2)}) copy-start(f32[2048,24]{0,1:T(8,128)} %param.17) | copy-start | bytes 589828
  16.4 8.8 %collective-permute-start.1 = (bf16[80,1536]{1,0:T(8,128)(2,1)S(1)}, bf16[80,1536]{1,0:T(8,128)(2,1)S(1)}, u32[]{:S(2)}, u32[]{:S(2)}) collective-permute-start(bf16[80,1536]{1,0:T(8,128)(2,1)S(1)} %shard_map.91.refs_0_), channel_id=1, source_target_pairs={{0,1},{1,0},{2,3},{3,2},{4,5},{5,4},{6,7},{7,6},{8,9},{9,8},{10,11... | collective-permute-start | bytes 737288 | tf_op jit(solution)/shard_map/ppermute | solution.py:375
  16.5 8.2 %collective-permute-start.9 = (bf16[40,1536]{1,0:T(8,128)(2,1)S(1)}, bf16[40,1536]{1,0:T(8,128)(2,1)S(1)}, u32[]{:S(2)}, u32[]{:S(2)}) collective-permute-start(bf16[40,1536]{1,0:T(8,128)(2,1)S(1)} %collective-permute-done.6.refs_0_), channel_id=1, source_target_pairs={{0,2},{1,3},{2,0},{3,1},{4,6},{5,7},{6,4},{7,5},{8,10},{9,11},{10,... | collective-permute-start | bytes 368648 | tf_op jit(solution)/shard_map/ppermute | solution.py:375
  18.8 6.0 %collective-permute-start.11 = (bf16[40,1536]{1,0:T(8,128)(2,1)S(1)}, bf16[40,1536]{1,0:T(8,128)(2,1)S(1)}, u32[]{:S(2)}, u32[]{:S(2)}) collective-permute-start(bf16[40,1536]{1,0:T(8,128)(2,1)S(1)} %collective-permute-done.7.refs_1_), channel_id=1, source_target_pairs={{0,2},{1,3},{2,0},{3,1},{4,6},{5,7},{6,4},{7,5},{8,10},{9,11},{10,... | collective-permute-start | bytes 368648 | tf_op jit(solution)/shard_map/ppermute | solution.py:375
  20.3 4.8 %collective-permute-start.3 = (bf16[80,1536]{1,0:T(8,128)(2,1)S(1)}, bf16[80,1536]{1,0:T(8,128)(2,1)S(1)}, u32[]{:S(2)}, u32[]{:S(2)}) collective-permute-start(bf16[80,1536]{1,0:T(8,128)(2,1)S(1)} %collective-permute-done.2.refs_2_), channel_id=1, source_target_pairs={{0,1},{1,0},{2,3},{3,2},{4,5},{5,4},{6,7},{7,6},{8,9},{9,8},{10,11... | collective-permute-start | bytes 737288 | tf_op jit(solution)/shard_map/ppermute | solution.py:375
  24.1 7.1 %collective-permute-start.8 = (bf16[80,1536]{1,0:T(8,128)(2,1)S(1)}, bf16[80,1536]{1,0:T(8,128)(2,1)S(1)}, u32[]{:S(2)}, u32[]{:S(2)}) collective-permute-start(bf16[80,1536]{1,0:T(8,128)(2,1)S(1)} %shard_map.99.refs_0_), channel_id=1, source_target_pairs={{0,1},{1,0},{2,3},{3,2},{4,5},{5,4},{6,7},{7,6},{8,9},{9,8},{10,11... | collective-permute-start | bytes 737288 | tf_op jit(solution)/shard_map/ppermute | solution.py:375
  24.7 6.5 %collective-permute-start.10 = (bf16[40,1536]{1,0:T(8,128)(2,1)S(1)}, bf16[40,1536]{1,0:T(8,128)(2,1)S(1)}, u32[]{:S(2)}, u32[]{:S(2)}) collective-permute-start(bf16[40,1536]{1,0:T(8,128)(2,1)S(1)} %collective-permute-done.9.refs_2_), channel_id=1, source_target_pairs={{0,1},{1,0},{2,3},{3,2},{4,5},{5,4},{6,7},{7,6},{8,9},{9,8},{10,11... | collective-permute-start | bytes 368648 | tf_op jit(solution)/shard_map/ppermute | solution.py:375
  24.8 6.3 %collective-permute-start.12 = (bf16[40,1536]{1,0:T(8,128)(2,1)S(1)}, bf16[40,1536]{1,0:T(8,128)(2,1)S(1)}, u32[]{:S(2)}, u32[]{:S(2)}) collective-permute-start(bf16[40,1536]{1,0:T(8,128)(2,1)S(1)} %collective-permute-done.11.refs_4_), channel_id=1, source_target_pairs={{0,1},{1,0},{2,3},{3,2},{4,5},{5,4},{6,7},{7,6},{8,9},{9,8},{10,11... | collective-permute-start | bytes 368648 | tf_op jit(solution)/shard_map/ppermute | solution.py:375
  31.0 18.7 %collective-permute-start.4 = (bf16[160,1536]{1,0:T(8,128)(2,1)S(1)}, bf16[160,1536]{1,0:T(8,128)(2,1)S(1)}, u32[]{:S(2)}, u32[]{:S(2)}) collective-permute-start(bf16[160,1536]{1,0:T(8,128)(2,1)S(1)} %shard_map.96), channel_id=1, source_target_pairs={{0,1},{1,0},{2,3},{3,2},{4,5},{5,4},{6,7},{7,6},{8,9},{9,8},{10,11... | collective-permute-start | bytes 1474568 | tf_op jit(solution)/shard_map/ppermute | solution.py:375
  36.7 1.8 %collective-permute-start.14 = (bf16[80,1536]{1,0:T(8,128)(2,1)S(1)}, bf16[80,1536]{1,0:T(8,128)(2,1)S(1)}, u32[]{:S(2)}, u32[]{:S(2)}) collective-permute-start(bf16[80,1536]{1,0:T(8,128)(2,1)S(1)} %get-tuple-element.38), channel_id=1, source_target_pairs={{0,1},{1,0},{2,3},{3,2},{4,5},{5,4},{6,7},{7,6},{8,9},{9,8},{10,11... | collective-permute-start | bytes 737288 | tf_op jit(solution)/shard_map/ppermute | solution.py:375
  37.2 4.8 %collective-permute-start.13 = (bf16[80,1536]{1,0:T(8,128)(2,1)S(1)}, bf16[80,1536]{1,0:T(8,128)(2,1)S(1)}, u32[]{:S(2)}, u32[]{:S(2)}) collective-permute-start(bf16[80,1536]{1,0:T(8,128)(2,1)S(1)} %get-tuple-element.36), channel_id=1, source_target_pairs={{0,1},{1,0},{2,3},{3,2},{4,5},{5,4},{6,7},{7,6},{8,9},{9,8},{10,11... | collective-permute-start | bytes 737288 | tf_op jit(solution)/shard_map/ppermute | solution.py:375
  38.5 14.8 %copy-start.4 = (s32[64,2]{0,1:T(2,128)S(1)}, s32[64,2]{0,1:T(2,128)}, u32[]{:S(2)}) copy-start(s32[64,2]{0,1:T(2,128)} %param.10) | copy-start | bytes 1540
  38.6 14.8 %copy-start.5 = (f32[64,2]{0,1:T(2,128)S(1)}, f32[64,2]{0,1:T(2,128)}, u32[]{:S(2)}) copy-start(f32[64,2]{0,1:T(2,128)} %param.11) | copy-start | bytes 1540
  38.6 6.3 %collective-permute-start.15 = (bf16[40,1536]{1,0:T(8,128)(2,1)S(1)}, bf16[40,1536]{1,0:T(8,128)(2,1)S(1)}, u32[]{:S(2)}, u32[]{:S(2)}) collective-permute-start(bf16[40,1536]{1,0:T(8,128)(2,1)S(1)} %shard_map.103), channel_id=1, source_target_pairs={{0,2},{1,3},{2,0},{3,1},{4,6},{5,7},{6,4},{7,5},{8,10},{9,11},{10,... | collective-permute-start | bytes 368648 | tf_op jit(solution)/shard_map/ppermute | solution.py:375
  39.2 8.6 %collective-permute-start.17 = (bf16[40,1536]{1,0:T(8,128)(2,1)S(1)}, bf16[40,1536]{1,0:T(8,128)(2,1)S(1)}, u32[]{:S(2)}, u32[]{:S(2)}) collective-permute-start(bf16[40,1536]{1,0:T(8,128)(2,1)S(1)} %shard_map.105), channel_id=1, source_target_pairs={{0,2},{1,3},{2,0},{3,1},{4,6},{5,7},{6,4},{7,5},{8,10},{9,11},{10,... | collective-permute-start | bytes 368648 | tf_op jit(solution)/shard_map/ppermute | solution.py:375
  44.9 11.2 %collective-permute-start.16 = (bf16[40,1536]{1,0:T(8,128)(2,1)S(1)}, bf16[40,1536]{1,0:T(8,128)(2,1)S(1)}, u32[]{:S(2)}, u32[]{:S(2)}) collective-permute-start(bf16[40,1536]{1,0:T(8,128)(2,1)S(1)} %shard_map.104), channel_id=1, source_target_pairs={{0,8},{1,9},{2,10},{3,11},{4,12},{5,13},{6,14},{7,15},{8,0},{9,1},... | collective-permute-start | bytes 368648 | tf_op jit(solution)/shard_map/ppermute | solution.py:375
  47.9 8.2 %collective-permute-start.18 = (bf16[40,1536]{1,0:T(8,128)(2,1)S(1)}, bf16[40,1536]{1,0:T(8,128)(2,1)S(1)}, u32[]{:S(2)}, u32[]{:S(2)}) collective-permute-start(bf16[40,1536]{1,0:T(8,128)(2,1)S(1)} %shard_map.106), channel_id=1, source_target_pairs={{0,12},{1,13},{2,14},{3,15},{4,8},{5,9},{6,10},{7,11},{8,4},{9,5},... | collective-permute-start | bytes 368648 | tf_op jit(solution)/shard_map/ppermute | solution.py:375
  49.8 8.4 %collective-permute-start.5 = (bf16[40,1536]{1,0:T(8,128)(2,1)S(1)}, bf16[40,1536]{1,0:T(8,128)(2,1)S(1)}, u32[]{:S(2)}, u32[]{:S(2)}) collective-permute-start(bf16[40,1536]{1,0:T(8,128)(2,1)S(1)} %get-tuple-element.33), channel_id=1, source_target_pairs={{0,4},{1,5},{2,6},{3,7},{4,0},{5,1},{6,2},{7,3},{8,12},{9,13},{10,... | collective-permute-start | bytes 368648 | tf_op jit(solution)/shard_map/ppermute | solution.py:375
  50.3 8.4 %collective-permute-start.19 = (bf16[40,1536]{1,0:T(8,128)(2,1)S(1)}, bf16[40,1536]{1,0:T(8,128)(2,1)S(1)}, u32[]{:S(2)}, u32[]{:S(2)}) collective-permute-start(bf16[40,1536]{1,0:T(8,128)(2,1)S(1)} %get-tuple-element.41), channel_id=1, source_target_pairs={{0,2},{1,3},{2,0},{3,1},{4,6},{5,7},{6,4},{7,5},{8,10},{9,11},{10,... | collective-permute-start | bytes 368648 | tf_op jit(solution)/shard_map/ppermute | solution.py:375
  50.8 9.0 %collective-permute-start.20 = (bf16[40,1536]{1,0:T(8,128)(2,1)S(1)}, bf16[40,1536]{1,0:T(8,128)(2,1)S(1)}, u32[]{:S(2)}, u32[]{:S(2)}) collective-permute-start(bf16[40,1536]{1,0:T(8,128)(2,1)S(1)} %get-tuple-element.42), channel_id=1, source_target_pairs={{0,6},{1,7},{2,4},{3,5},{4,2},{5,3},{6,0},{7,1},{8,14},{9,15},{10,... | collective-permute-start | bytes 368648 | tf_op jit(solution)/shard_map/ppermute | solution.py:375
